TPU v7x, 16 devices: a whole 2x2x2 slice. The times are simulated.
16 devices in a mesh: fsdp: 16 (over z, y, x, core).
Axes of the slice: x: 2, y: 2, z: 2, core: 2. Of those that a mesh axis runs over, the one named last changes fastest.
Arguments:
- x_saved: bfloat16 [2, 32, 1536, 1024], P(None, 'fsdp')
- grad_out: bfloat16 [32, 1536, 1024], P('fsdp')
- x_next: bfloat16 [32, 1536, 1024], P('fsdp')
- w_up: bfloat16 [2, 1024, 4096], replicated
- w_down: bfloat16 [2, 4096, 1024], replicated
- gacc_up: float32 [2, 1024, 4096], P(None, 'fsdp')
- gacc_down: float32 [2, 4096, 1024], P(None, 'fsdp')
- master_up: float32 [2, 1024, 4096], P(None, 'fsdp')
- master_down: float32 [2, 4096, 1024], P(None, 'fsdp')
- mom1_up: float32 [2, 1024, 4096], P(None, 'fsdp')
- mom1_down: float32 [2, 4096, 1024], P(None, 'fsdp')
- mom2_up: float32 [2, 1024, 4096], P(None, 'fsdp')
- mom2_down: float32 [2, 4096, 1024], P(None, 'fsdp')
Outputs:
- output 1: bfloat16 [32, 1536, 1024], P('fsdp')
- output 2: float32 [2, 1024, 4096], P(None, 'fsdp')
- output 3: float32 [2, 4096, 1024], P(None, 'fsdp')
- output 4: float32 [2, 1024, 4096], P(None, 'fsdp')
- output 5: float32 [2, 4096, 1024], P(None, 'fsdp')
- output 6: float32 [2, 1024, 4096], P(None, 'fsdp')
- output 7: float32 [2, 4096, 1024], P(None, 'fsdp')
All inputs are finite; a program needn't handle non-finite values.
Results may differ from a plain program's by a relative error of at most 0.00842076.
Values are sent between devices in bfloat16 or wider.
A program may use at most 1 GiB of HBM per device.

v0:
```python
import math
import jax
import jax.numpy as jnp
from jax import lax
from jax.sharding import PartitionSpec as P

LEARN_RATE = 0.001
BETA_ONE = 0.9
BETA_TWO = 0.95
ADAM_EPS = 1e-8
WEIGHT_DECAY = 0.1
ADAM_STEP = 3
MICRO_STEPS = 2


def gelu_fn(pre_act):
    return jax.nn.gelu(pre_act, approximate=True)


def adamw_update(master_old, mom_one, mom_two, grad_clip):
    mom_one_new = BETA_ONE * mom_one + (1.0 - BETA_ONE) * grad_clip
    mom_two_new = BETA_TWO * mom_two + (1.0 - BETA_TWO) * grad_clip * grad_clip
    first_hat = mom_one_new / (1.0 - BETA_ONE ** ADAM_STEP)
    second_hat = mom_two_new / (1.0 - BETA_TWO ** ADAM_STEP)
    master_new = master_old - LEARN_RATE * (first_hat / (jnp.sqrt(second_hat) + ADAM_EPS) + WEIGHT_DECAY * master_old)
    return master_new, mom_one_new, mom_two_new


def reduce_rows(part_grad, n_dev):
    received = lax.all_to_all(part_grad, "fsdp", 0, 0, tiled=True)
    return jnp.sum(received.reshape(n_dev, -1, part_grad.shape[1]), axis=0, dtype=jnp.float32)


def backward_update(x_saved, grad_out, w_up, w_down, gacc_up, gacc_down, master_up, master_down, mom1_up, mom1_down, mom2_up, mom2_down, n_dev):
    layers, model_width, ff_width = w_up.shape
    clip_norm = 0.1 * math.sqrt(2 * layers * model_width * ff_width)
    x_tokens = x_saved.reshape(layers, -1, model_width)
    grad_cur = grad_out.reshape(-1, model_width)
    sums_up = []
    sums_down = []
    for layer_idx in range(layers - 1, -1, -1):
        x_in = x_tokens[layer_idx]
        pre_act = jnp.dot(x_in, w_up[layer_idx], preferred_element_type=jnp.float32)
        hidden_act, gelu_vjp = jax.vjp(gelu_fn, pre_act)
        d_act = lax.dot_general(grad_cur, w_down[layer_idx], (((1,), (1,)), ((), ())), preferred_element_type=jnp.float32)
        d_pre = gelu_vjp(d_act)[0].astype(jnp.bfloat16)
        part_down = lax.dot_general(hidden_act.astype(jnp.bfloat16), grad_cur, (((0,), (0,)), ((), ())), preferred_element_type=jnp.float32).astype(jnp.bfloat16)
        part_up = lax.dot_general(x_in, d_pre, (((0,), (0,)), ((), ())), preferred_element_type=jnp.float32).astype(jnp.bfloat16)
        if layer_idx > 0:
            grad_cur = (grad_cur.astype(jnp.float32) + lax.dot_general(d_pre, w_up[layer_idx], (((1,), (1,)), ((), ())), preferred_element_type=jnp.float32)).astype(jnp.bfloat16)
        sums_down.append(reduce_rows(part_down, n_dev))
        sums_up.append(reduce_rows(part_up, n_dev))
    grad_up = (gacc_up + jnp.stack(sums_up[::-1])) / MICRO_STEPS
    grad_down = (gacc_down + jnp.stack(sums_down[::-1])) / MICRO_STEPS
    local_sq = jnp.sum(grad_up * grad_up) + jnp.sum(grad_down * grad_down)
    clip_factor = jnp.minimum(1.0, clip_norm / jnp.sqrt(lax.psum(local_sq, "fsdp")))
    new_up = adamw_update(master_up, mom1_up, mom2_up, grad_up * clip_factor)
    new_down = adamw_update(master_down, mom1_down, mom2_down, grad_down * clip_factor)
    return new_up, new_down


def solution(mesh):
    n_dev = mesh.shape["fsdp"]
    rows_spec = P(None, "fsdp")

    def local_step(x_saved, grad_out, x_next, w_up, w_down, gacc_up, gacc_down, master_up, master_down, mom1_up, mom1_down, mom2_up, mom2_down):
        new_up, new_down = backward_update(x_saved, grad_out, w_up, w_down, gacc_up, gacc_down, master_up, master_down, mom1_up, mom1_down, mom2_up, mom2_down, n_dev)
        up_shard = new_up[0].astype(jnp.bfloat16)
        down_shard = new_down[0].astype(jnp.bfloat16)
        hidden_state = x_next.reshape(-1, x_next.shape[2])
        for layer_idx in range(up_shard.shape[0]):
            w_layer_up = lax.all_gather(up_shard[layer_idx], "fsdp", axis=0, tiled=True)
            w_layer_down = lax.all_gather(down_shard[layer_idx], "fsdp", axis=0, tiled=True)
            pre_act = jnp.dot(hidden_state, w_layer_up, preferred_element_type=jnp.float32)
            hidden_act = gelu_fn(pre_act).astype(jnp.bfloat16)
            hidden_state = (hidden_state.astype(jnp.float32) + jnp.dot(hidden_act, w_layer_down, preferred_element_type=jnp.float32)).astype(jnp.bfloat16)
        return (hidden_state.reshape(x_next.shape), new_up[0], new_down[0], new_up[1], new_down[1], new_up[2], new_down[2])

    return jax.shard_map(local_step, mesh=mesh, in_specs=(rows_spec, P("fsdp"), P("fsdp"), P(), P(), rows_spec, rows_spec, rows_spec, rows_spec, rows_spec, rows_spec, rows_spec, rows_spec), out_specs=(P("fsdp"), rows_spec, rows_spec, rows_spec, rows_spec, rows_spec, rows_spec), check_vma=False)
```

profile of v0, /device:TPU:0, one launch (start us, length us, event | category | flops | bytes accessed | tf_op | source)
XLA Modules:
  0.0 854.9 jit_solution(2661285231566406906)
XLA Ops:
  7.2 0.0 slice-start.4
  7.2 8.6 %fusion.97 = (bf16[1,2,1536,1024]{3,2,1,0:T(8,128)(2,1)}, bf16[1,2,1536,1024]{3,2,1,0:T(8,128)(2,1)S(1)}) fusion(bf16[2,2,1536,1024]{3,2,1,0:T(8,128)(2,1)} %param.13), kind=kLoop, calls=%fused_computation.106 | loop fusion | bytes 25165824 | tf_op jit(solution)/shard_map/slice | solution.py:42
  15.8 35.3 %fusion.43 = f32[3072,4096]{1,0:T(8,128)} fusion(bf16[3072,1024]{1,0:T(8,128)(2,1)S(1)} %bitcast.123, bf16[2,1024,4096]{2,1,0:T(8,128)(2,1)} %param.16), kind=kOutput, calls=%fused_computation.58 | convolution fusion | flops 25769803776 | bytes 65011712 | tf_op jit(solution)/shard_map/dot_general | solution.py:43
  51.1 40.3 %fusion.49 = bf16[4096,1024]{1,0:T(8,128)(2,1)} fusion(bf16[3072,1024]{1,0:T(8,128)(2,1)S(1)} %bitcast.131, f32[3072,4096]{1,0:T(8,128)} %fusion.43), kind=kOutput, calls=%fused_computation.64 | convolution fusion | flops 25887244288 | bytes 65011712 | tf_op jit(solution)/shard_map/dot_general | solution.py:47
  91.5 5.6 all-to-all-start.3
  97.1 64.1 %fusion.6 = bf16[3072,4096]{1,0:T(8,128)(2,1)} fusion(f32[3072,4096]{1,0:T(8,128)} %fusion.43, bf16[3072,1024]{1,0:T(8,128)(2,1)} %bitcast.127, bf16[2,4096,1024]{2,1,0:T(8,128)(2,1)} %param.17), kind=kOutput, calls=%fused_computation.12 | convolution fusion | flops 26021462016 | bytes 90177536 | tf_op jit(solution)/shard_map/dot_general | solution.py:45
  161.2 31.5 %convolution_convert_fusion = bf16[4096,1024]{0,1:T(8,128)(2,1)} fusion(bf16[3072,4096]{1,0:T(8,128)(2,1)} %fusion.6, bf16[3072,1024]{1,0:T(8,128)(2,1)S(1)} %bitcast.126), kind=kOutput, calls=%fused_computation.66 | convolution fusion | flops 25773998080 | bytes 39845888 | tf_op jit(solution)/shard_map/dot_general | solution.py:48
  192.7 33.5 %add_convert_fusion.2 = bf16[3072,1024]{1,0:T(8,128)(2,1)} fusion(bf16[3072,1024]{1,0:T(8,128)(2,1)} %bitcast.128, bf16[3072,4096]{1,0:T(8,128)(2,1)} %fusion.6, bf16[2,1024,4096]{2,1,0:T(8,128)(2,1)} %param.16), kind=kOutput, calls=%fused_computation.46 | convolution fusion | flops 25779240960 | bytes 46137344 | tf_op jit(solution)/shard_map/dot_general | solution.py:50
  226.3 4.5 all-to-all-start.1
  230.8 35.0 %fusion.38 = f32[3072,4096]{1,0:T(8,128)} fusion(bf16[3072,1024]{1,0:T(8,128)(2,1)} %bitcast.119, bf16[2,1024,4096]{2,1,0:T(8,128)(2,1)} %param.16), kind=kOutput, calls=%fused_computation.53 | convolution fusion | flops 25769803776 | bytes 65011712 | tf_op jit(solution)/shard_map/dot_general | solution.py:43
  265.8 39.7 %fusion.50 = bf16[4096,1024]{1,0:T(8,128)(2,1)} fusion(bf16[3072,1024]{1,0:T(8,128)(2,1)S(1)} %bitcast.136, f32[3072,4096]{1,0:T(8,128)} %fusion.38), kind=kOutput, calls=%fused_computation.65 | convolution fusion | flops 25887244288 | bytes 65011712 | tf_op jit(solution)/shard_map/dot_general | solution.py:47
  305.5 32.2 %all-to-all-done.1 = bf16[16,64,4096]{2,1,0:T(8,128)(2,1)} async-done(((bf16[16,64,4096]{2,1,0:T(8,128)(2,1)}), bf16[16,64,4096]{2,1,0:T(8,128)(2,1)}, u32[]{:S(2)}, u32[]{:S(2)}) %all-to-all-start.1) | async-done | bytes 8388640 | tf_op jit(solution)/shard_map/all_to_all | solution.py:30
  337.7 4.2 all-to-all-start.2
  341.9 0.0 slice-start.1
  341.9 64.1 %fusion.13.clone.4 = bf16[3072,4096]{1,0:T(8,128)(2,1)} fusion(f32[3072,4096]{1,0:T(8,128)} %fusion.38, bf16[3072,1024]{1,0:T(8,128)(2,1)} %add_convert_fusion.2, bf16[2,4096,1024]{2,1,0:T(8,128)(2,1)} %param.17), kind=kOutput, calls=%fused_computation.19.clone.clone.clone.1 | convolution fusion | flops 26021462016 | bytes 90177536 | tf_op jit(solution)/shard_map/dot_general | solution.py:45
  406.0 31.5 %convolution_convert_fusion.1 = bf16[4096,1024]{0,1:T(8,128)(2,1)} fusion(bf16[3072,1024]{1,0:T(8,128)(2,1)S(1)} %bitcast.122, bf16[3072,4096]{1,0:T(8,128)(2,1)} %fusion.13.clone.4), kind=kOutput, calls=%fused_computation.67 | convolution fusion | flops 25773998080 | bytes 39845888 | tf_op jit(solution)/shard_map/dot_general | solution.py:48
  437.6 11.2 %all-to-all-done.2 = bf16[16,256,1024]{2,1,0:T(8,128)(2,1)} async-done(((bf16[16,256,1024]{2,1,0:T(8,128)(2,1)}), bf16[16,256,1024]{2,1,0:T(8,128)(2,1)}, u32[]{:S(2)}, u32[]{:S(2)}) %all-to-all-start.2) | async-done | bytes 8388640 | tf_op jit(solution)/shard_map/all_to_all | solution.py:30
  448.8 4.0 all-to-all-start
  452.8 0.5 all-gather.9.cloned.1.call-start
  453.3 0.0 copy-start.2
  453.3 5.6 convert_reduce_fusion
  459.0 5.5 convert_reduce_fusion.1
  464.5 1.2 multiply_reduce_fusion
  465.7 5.0 convert_reduce_fusion.2
  470.7 89.0 %all-to-all-done = bf16[16,64,4096]{2,1,0:T(8,128)(2,1)} async-done(((bf16[16,64,4096]{2,1,0:T(8,128)(2,1)}), bf16[16,64,4096]{2,1,0:T(8,128)(2,1)}, u32[]{:S(2)}, u32[]{:S(2)}) %all-to-all-start) | async-done | bytes 8388640 | tf_op jit(solution)/shard_map/all_to_all | solution.py:30
  559.7 5.2 convert_reduce_fusion.3
  565.0 1.0 copy-done
  565.9 1.2 multiply_reduce_fusion.1
  568.4 33.2 %psum.7 = f32[]{:T(128)} all-reduce(f32[]{:T(128)S(6)} %add.83), channel_id=1, replica_groups=mesh['fsdp'=16] {'fsdp'}, use_global_device_ids=true, to_apply=%region_6.0 | all-reduce | flops 1 | bytes 8 | tf_op jit(solution)/shard_map/psum | solution.py:56
  602.3 7.8 fusion.93
  610.1 1.1 fusion.98
  611.1 0.0 all-gather.9.cloned.1.call-update
  611.2 0.0 all-gather.11.cloned.1.call-start
  611.2 7.6 fusion.95
  618.9 1.0 fusion.99
  619.9 0.0 all-gather.11.cloned.1.call-update
  619.9 0.0 all-gather.13.cloned.1.call-start
  620.0 0.7 all-gather.13.cloned.1.call-update
  620.7 0.3 all-gather.15.cloned.1.call-start
  620.9 0.3 all-gather.15.cloned.1.call-update
  621.2 39.9 %all-gather.9.cloned.1.call-done = bf16[1,1024,4096]{2,1,0:T(8,128)(2,1)} async-done(((bf16[1,64,4096]{2,1,0:T(8,128)(2,1)}), bf16[1,1024,4096]{2,1,0:T(8,128)(2,1)}) %all-gather.9.cloned.1.call-update) | async-done | bytes 8388624 | tf_op jit(solution)/shard_map/all_gather | solution.py:72
  661.1 41.0 %fusion.21.clone.6 = bf16[3072,4096]{1,0:T(8,128)(2,1)} fusion(bf16[3072,1024]{1,0:T(8,128)(2,1)} %bitcast.132, bf16[1,1024,4096]{2,1,0:T(8,128)(2,1)} %all-gather.9.cloned.1.call-done), kind=kOutput, calls=%fused_computation.27.clone.clone.clone.clone.clone.1 | convolution fusion | flops 25883049984 | bytes 39845888 | tf_op jit(solution)/shard_map/dot_general | solution.py:74
  702.1 10.5 %all-gather.11.cloned.1.call-done = bf16[1,4096,1024]{2,1,0:T(8,128)(2,1)} async-done(((bf16[1,256,1024]{2,1,0:T(8,128)(2,1)}), bf16[1,4096,1024]{2,1,0:T(8,128)(2,1)}) %all-gather.11.cloned.1.call-update) | async-done | bytes 8388624 | tf_op jit(solution)/shard_map/all_gather | solution.py:73
  712.6 33.5 %add_convert_fusion.1 = bf16[3072,1024]{1,0:T(8,128)(2,1)} fusion(bf16[3072,1024]{1,0:T(8,128)(2,1)} %bitcast.133, bf16[1,4096,1024]{2,1,0:T(8,128)(2,1)} %all-gather.11.cloned.1.call-done, bf16[3072,4096]{1,0:T(8,128)(2,1)} %fusion.21.clone.6), kind=kOutput, calls=%fused_computation.45 | convolution fusion | flops 25779240960 | bytes 46137344 | tf_op jit(solution)/shard_map/dot_general | solution.py:76
  746.1 17.4 %all-gather.13.cloned.1.call-done = bf16[1,1024,4096]{2,1,0:T(8,128)(2,1)} async-done(((bf16[1,64,4096]{2,1,0:T(8,128)(2,1)}), bf16[1,1024,4096]{2,1,0:T(8,128)(2,1)}) %all-gather.13.cloned.1.call-update) | async-done | bytes 8388624 | tf_op jit(solution)/shard_map/all_gather | solution.py:72
  763.6 41.0 %fusion.29.clone.6 = bf16[3072,4096]{1,0:T(8,128)(2,1)} fusion(bf16[3072,1024]{1,0:T(8,128)(2,1)} %add_convert_fusion.1, bf16[1,1024,4096]{2,1,0:T(8,128)(2,1)} %all-gather.13.cloned.1.call-done), kind=kOutput, calls=%fused_computation.35.clone.clone.clone.clone.clone.1 | convolution fusion | flops 25883049984 | bytes 39845888 | tf_op jit(solution)/shard_map/dot_general | solution.py:74
  804.5 9.8 %all-gather.15.cloned.1.call-done = bf16[1,4096,1024]{2,1,0:T(8,128)(2,1)} async-done(((bf16[1,256,1024]{2,1,0:T(8,128)(2,1)}), bf16[1,4096,1024]{2,1,0:T(8,128)(2,1)}) %all-gather.15.cloned.1.call-update) | async-done | bytes 8388624 | tf_op jit(solution)/shard_map/all_gather | solution.py:73
  814.3 33.5 %add_convert_fusion = bf16[3072,1024]{1,0:T(8,128)(2,1)} fusion(bf16[3072,1024]{1,0:T(8,128)(2,1)} %add_convert_fusion.1, bf16[1,4096,1024]{2,1,0:T(8,128)(2,1)} %all-gather.15.cloned.1.call-done, bf16[3072,4096]{1,0:T(8,128)(2,1)} %fusion.29.clone.6), kind=kOutput, calls=%fused_computation.44 | convolution fusion | flops 25779240960 | bytes 46137344 | tf_op jit(solution)/shard_map/dot_general | solution.py:76
  (25 shorter events, 0.0 us)
Async XLA Ops:
  7.2 43.9 %slice-start.4 = ((s8[6291456]{0:T(1024)(128)(4,1)}), s8[4194304]{0:T(1024)(128)(4,1)S(1)}, s32[]{:S(2)}) async-start(s8[6291456]{0:T(1024)(128)(4,1)} %bitcast.129), calls=%async_computation.12 | async-start | bytes 8388608
  15.8 35.4 %copy-start.3 = (bf16[1,2,1536,1024]{3,2,1,0:T(8,128)(2,1)}, bf16[1,2,1536,1024]{3,2,1,0:T(8,128)(2,1)S(1)}, u32[]{:S(2)}) copy-start(bf16[1,2,1536,1024]{3,2,1,0:T(8,128)(2,1)S(1)} %get-tuple-element.16) | copy-start | bytes 18874372
  15.8 35.4 %slice-start.5 = ((s8[6291456]{0:T(1024)(128)(4,1)}), s8[2097152]{0:T(1024)(128)(4,1)S(1)}, s32[]{:S(2)}) async-start(s8[6291456]{0:T(1024)(128)(4,1)} %bitcast.129), calls=%async_computation.13 | async-start | bytes 4194304
  91.5 69.7 %slice-start.2 = ((s8[6291456]{0:T(1024)(128)(4,1)}), s8[2097152]{0:T(1024)(128)(4,1)S(1)}, s32[]{:S(2)}) async-start(s8[6291456]{0:T(1024)(128)(4,1)} %bitcast.124), calls=%async_computation.10 | async-start | bytes 4194304
  91.5 134.8 %all-to-all-start.3 = ((bf16[16,256,1024]{2,1,0:T(8,128)(2,1)}), bf16[16,256,1024]{2,1,0:T(8,128)(2,1)}, u32[]{:S(2)}, u32[]{:S(2)}) async-start(bf16[16,256,1024]{2,1,0:T(8,128)(2,1)} %bitcast.118), calls=%async_computation.3 | async-start | bytes 16777216 | tf_op jit(solution)/shard_map/all_to_all | solution.py:30
  97.1 64.1 %slice-start.3 = ((s8[6291456]{0:T(1024)(128)(4,1)}), s8[4194304]{0:T(1024)(128)(4,1)S(1)}, s32[]{:S(2)}) async-start(s8[6291456]{0:T(1024)(128)(4,1)} %bitcast.124), calls=%async_computation.11 | async-start | bytes 8388608
  226.3 39.5 %slice-start.6 = ((s8[6291456]{0:T(1024)(128)(4,1)}), s8[2097152]{0:T(1024)(128)(4,1)S(1)}, s32[]{:S(2)}) async-start(s8[6291456]{0:T(1024)(128)(4,1)} %bitcast.135), calls=%async_computation.14 | async-start | bytes 4194304
  226.3 111.4 %all-to-all-start.1 = ((bf16[16,64,4096]{2,1,0:T(8,128)(2,1)}), bf16[16,64,4096]{2,1,0:T(8,128)(2,1)}, u32[]{:S(2)}, u32[]{:S(2)}) async-start(bf16[16,64,4096]{2,1,0:T(8,128)(2,1)} %bitcast.116), calls=%async_computation.1 | async-start | bytes 16777216 | tf_op jit(solution)/shard_map/all_to_all | solution.py:30
  230.8 35.1 %slice-start.7 = ((s8[6291456]{0:T(1024)(128)(4,1)}), s8[4194304]{0:T(1024)(128)(4,1)S(1)}, s32[]{:S(2)}) async-start(s8[6291456]{0:T(1024)(128)(4,1)} %bitcast.135), calls=%async_computation.15 | async-start | bytes 8388608
  337.7 68.4 %slice-start = ((s8[6291456]{0:T(1024)(128)(4,1)}), s8[2097152]{0:T(1024)(128)(4,1)S(1)}, s32[]{:S(2)}) async-start(s8[6291456]{0:T(1024)(128)(4,1)} %bitcast.120), calls=%async_computation.8 | async-start | bytes 4194304
  337.7 111.1 %all-to-all-start.2 = ((bf16[16,256,1024]{2,1,0:T(8,128)(2,1)}), bf16[16,256,1024]{2,1,0:T(8,128)(2,1)}, u32[]{:S(2)}, u32[]{:S(2)}) async-start(bf16[16,256,1024]{2,1,0:T(8,128)(2,1)} %bitcast.117), calls=%async_computation.2 | async-start | bytes 16777216 | tf_op jit(solution)/shard_map/all_to_all | solution.py:30
  341.9 64.1 %slice-start.1 = ((s8[6291456]{0:T(1024)(128)(4,1)}), s8[4194304]{0:T(1024)(128)(4,1)S(1)}, s32[]{:S(2)}) async-start(s8[6291456]{0:T(1024)(128)(4,1)} %bitcast.120), calls=%async_computation.9 | async-start | bytes 8388608
  448.8 110.9 %all-to-all-start = ((bf16[16,64,4096]{2,1,0:T(8,128)(2,1)}), bf16[16,64,4096]{2,1,0:T(8,128)(2,1)}, u32[]{:S(2)}, u32[]{:S(2)}) async-start(bf16[16,64,4096]{2,1,0:T(8,128)(2,1)} %bitcast.115), calls=%async_computation | async-start | bytes 16777216 | tf_op jit(solution)/shard_map/all_to_all | solution.py:30
  452.8 208.3 %all-gather.9.cloned.1.call-start = ((), (), s32[]{:S(2)}) async-start(), calls=%async_computation.4 | async-start | bytes 8912896 | tf_op jit(solution)/shard_map/all_gather | solution.py:72
  453.3 11.2 %copy-start.2 = (f32[2,256,1024]{2,1,0:T(8,128)S(1)}, f32[2,256,1024]{2,1,0:T(8,128)}, u32[]{:S(2)}) copy-start(f32[2,256,1024]{2,1,0:T(8,128)} %param.19) | copy-start | bytes 6291460
  559.7 6.2 copy-start.1
  564.9 1.0 copy-start
  611.2 101.5 %all-gather.11.cloned.1.call-start = ((), (), s32[]{:S(2)}) async-start(), calls=%async_computation.5 | async-start | bytes 8912896 | tf_op jit(solution)/shard_map/all_gather | solution.py:73
  619.9 143.6 %all-gather.13.cloned.1.call-start = ((), (), s32[]{:S(2)}) async-start(), calls=%async_computation.6 | async-start | bytes 8912896 | tf_op jit(solution)/shard_map/all_gather | solution.py:72
  620.7 193.7 %all-gather.15.cloned.1.call-start = ((), (), s32[]{:S(2)}) async-start(), calls=%async_computation.7 | async-start | bytes 8912896 | tf_op jit(solution)/shard_map/all_gather | solution.py:73
Sparse Core Ops, SparseCore 0:
  611.3 49.8 all-gather.8
  663.9 48.6 all-gather.10
  714.9 48.6 all-gather.12
  765.7 48.6 all-gather.14
where the time goes:
time: 861 us; the launch traced here: 855 us
  matrix products  524 us (61%)
  waiting for transfers between devices  211 us (25%)
  other arithmetic  39.2 us (5%)
  blocking collectives  33.2 us (4%)
  starting transfers between devices  19.1 us (2%)
  between operations  16.4 us (2%)
  local copies, waits for them, and re-layouts  11.7 us (1%)
    all_to_all x4, waiting for transfers between devices, reduce_rows(): received = lax.all_to_all(part_grad, 'fsdp', 0, 0, tiled=True)  132 us
    dot_general x2, matrix products, backward_update(): lax.dot_general(grad_cur, w_down[layer_idx], (((1,), (1,)), ((), ())), pr...  128 us
    dot_general x2, matrix products, local_step(): jnp.dot(hidden_state, w_layer_up, preferred_element_type=jnp.float32)  81.9 us
    dot_general x2, matrix products, backward_update(): lax.dot_general(hidden_act.astype(jnp.bfloat16), grad_cur, (((0,), (0,)),...  80 us
    dot_general x2, matrix products, backward_update(): pre_act = jnp.dot(x_in, w_up[layer_idx], preferred_element_type=jnp.float32)  70.4 us
    dot_general x2, matrix products, local_step(): jnp.dot(hidden_act, w_layer_down, preferred_element_type=jnp.float32)  67 us
    dot_general x2, matrix products, backward_update(): lax.dot_general(x_in, d_pre, (((0,), (0,)), ((), ())), preferred_element_...  63.1 us
    all_gather x2, waiting for transfers between devices, local_step(): w_layer_up = lax.all_gather(up_shard[layer_idx], 'fsdp', axis=0, tiled=True)  57.3 us
  transfers between devices with their start and end apart: 8, of which 7 were waited for; matrix products, arithmetic and copies ran while one was open for 52% of the time, Pallas kernels for 0%

commit v1 on v0

v1 whole, which is shorter than its diff:
```python
import functools
import math
import jax
import jax.numpy as jnp
from jax import lax
from jax.experimental import pallas as pl
from jax.experimental.pallas import tpu as pltpu
from jax.sharding import PartitionSpec as P

LEARN_RATE = 0.001
BETA_ONE = 0.9
BETA_TWO = 0.95
ADAM_EPS = 1e-8
WEIGHT_DECAY = 0.1
ADAM_STEP = 3
MICRO_STEPS = 2

GELU_A = math.sqrt(2.0 / math.pi)
GELU_B = GELU_A * 0.044715
MESH = pl.DeviceIdType.MESH
STRIDES = (8, 4, 2, 1)
ORDERS = ((2, 1, 0), (1, 0, 2), (0, 2, 1))
TILE = 512


def gelu_fn(pre_act):
    return jax.nn.gelu(pre_act, approximate=True)


def adamw_update(master_old, mom_one, mom_two, grad_clip):
    mom_one_new = BETA_ONE * mom_one + (1.0 - BETA_ONE) * grad_clip
    mom_two_new = BETA_TWO * mom_two + (1.0 - BETA_TWO) * grad_clip * grad_clip
    first_hat = mom_one_new / (1.0 - BETA_ONE ** ADAM_STEP)
    second_hat = mom_two_new / (1.0 - BETA_TWO ** ADAM_STEP)
    master_new = master_old - LEARN_RATE * (first_hat / (jnp.sqrt(second_hat) + ADAM_EPS) + WEIGHT_DECAY * master_old)
    return master_new, mom_one_new, mom_two_new


def dot_nt(left, right):
    return lax.dot_general(left, right, (((1,), (1,)), ((), ())), preferred_element_type=jnp.float32)


def dot_tn(left, right):
    return lax.dot_general(left, right, (((0,), (0,)), ((), ())), preferred_element_type=jnp.float32)


def at_bits(picks, count):
    return tuple(picks.get(dim, slice(None)) for dim in range(count))


def backward_kernel(n_steps, n_chunks, cols, x_hbm, g_hbm, w1_ref, w2_ref, out1_ref, out2_ref, x_buf, g_buf, acc, act_buf, dh_buf, part1, part2, *rest):
    parts = (part1, part2)
    recv0, send1, keep1, recv1, send2, keep2, recv2, send3, keep3, recv3 = (rest[2 * i:2 * i + 2] for i in range(10))
    load_sem, send_sem0, recv_sem0, send_sem, recv_sem = rest[20:]
    outs = (out1_ref, out2_ref)
    step = pl.program_id(0)
    me = lax.axis_index("fsdp")
    bits = [lax.rem(me // stride, 2) for stride in STRIDES]
    peers = [me + (1 - 2 * bit) * stride for bit, stride in zip(bits, STRIDES)]
    tokens = x_buf.shape[0]
    sends = (send1, send2, send3)
    recvs = (recv1, recv2, recv3)

    def core_copy(mat, block):
        return pltpu.make_async_remote_copy(
            src_ref=parts[mat].at[:, :, :, 1 - bits[3]], dst_ref=recv0[mat].at[lax.rem(block, 2)],
            send_sem=send_sem0.at[mat], recv_sem=recv_sem0.at[mat, lax.rem(block, 2)],
            device_id=(peers[3],), device_id_type=MESH)

    def axis_copy(phase, mat, color, block):
        lo, hi = cols[mat][color]
        lead = (slice(None),) * (4 - phase)
        slot = (phase - 1) * 6 + mat * 3 + color
        return pltpu.make_async_remote_copy(
            src_ref=sends[phase - 1][mat].at[lead + (pl.ds(lo, hi - lo),)],
            dst_ref=recvs[phase - 1][mat].at[(lax.rem(block, 2),) + lead + (pl.ds(lo, hi - lo),)],
            send_sem=send_sem.at[slot], recv_sem=recv_sem.at[slot, lax.rem(block, 2)],
            device_id=(peers[ORDERS[color][phase - 1]],), device_id_type=MESH)

    def each_color():
        for mat in range(2):
            for color in range(3):
                yield mat, color, pl.ds(cols[mat][color][0], cols[mat][color][1] - cols[mat][color][0])

    @pl.when(step == 0)
    def _():
        barrier = pltpu.get_barrier_semaphore()
        for peer in peers:
            pl.semaphore_signal(barrier, inc=1, device_id=(peer,), device_id_type=MESH)
        load_x = pltpu.make_async_copy(x_hbm.at[1], x_buf, load_sem.at[0])
        load_g = pltpu.make_async_copy(g_hbm, g_buf, load_sem.at[1])
        load_x.start()
        load_g.start()
        acc[...] = jnp.zeros_like(acc)
        load_x.wait()
        load_g.wait()
        pl.semaphore_wait(barrier, 4)

    @pl.when(step == n_chunks)
    def _():
        load_x = pltpu.make_async_copy(x_hbm.at[0], x_buf, load_sem.at[0])
        load_x.start()
        load_x.wait()

    @pl.when(step < n_steps)
    def _():
        def tile_body(tile, carry):
            rows = pl.ds(pl.multiple_of(tile * TILE, TILE), TILE)
            pre = jnp.dot(x_buf[rows, :], w1_ref[...], preferred_element_type=jnp.float32)
            d_act = dot_nt(g_buf[rows, :], w2_ref[...].reshape(w1_ref.shape[1], w1_ref.shape[0]))
            square = pre * pre
            gate = 0.5 + 0.5 * jnp.tanh(pre * (GELU_A + GELU_B * square))
            act = pre * gate
            act_buf[rows, :] = act.astype(jnp.bfloat16)
            slope = gate + (act * (1.0 - gate)) * (2.0 * GELU_A + 6.0 * GELU_B * square)
            dh_buf[rows, :] = (d_act * slope).astype(jnp.bfloat16)
            return carry
        lax.fori_loop(0, tokens // TILE, tile_body, 0)

    @pl.when(step >= 4)
    def _():
        block = step - 4
        for mat, color, span in each_color():
            copy = axis_copy(3, mat, color, block)
            copy.wait_send()
            copy.wait_recv()
            outs[mat][:, span] = keep3[mat][:, span] + recv3[mat][lax.rem(block, 2), :, span]

    @pl.when((step >= 3) & (step < n_steps + 3))
    def _():
        block = step - 3
        for mat, color, span in each_color():
            copy = axis_copy(2, mat, color, block)
            copy.wait_send()
            copy.wait_recv()
            bit = bits[ORDERS[color][2]]
            slot = lax.rem(block, 2)
            send3[mat][:, span] = keep2[mat][1 - bit, :, span] + recv2[mat][slot, 1 - bit, :, span]
            keep3[mat][:, span] = keep2[mat][bit, :, span] + recv2[mat][slot, bit, :, span]
            axis_copy(3, mat, color, block).start()

    @pl.when((step >= 2) & (step < n_steps + 2))
    def _():
        block = step - 2
        for mat, color, span in each_color():
            copy = axis_copy(1, mat, color, block)
            copy.wait_send()
            copy.wait_recv()
            left = [axis for axis in range(3) if axis != ORDERS[color][0]]
            place = left.index(ORDERS[color][1])
            bit = bits[ORDERS[color][1]]
            slot = lax.rem(block, 2)
            for value, store in ((1 - bit, send2), (bit, keep2)):
                index = at_bits({place: value}, 2)
                store[mat][:, :, span] = keep1[mat][index + (slice(None), span)] + recv1[mat][(slot,) + index + (slice(None), span)]
            axis_copy(2, mat, color, block).start()

    @pl.when((step >= 1) & (step < n_steps + 1))
    def _():
        block = step - 1
        for mat in range(2):
            copy = core_copy(mat, block)
            copy.wait_send()
            copy.wait_recv()
        for mat, color, span in each_color():
            axis = ORDERS[color][0]
            slot = lax.rem(block, 2)
            for value, store in ((1 - bits[axis], send1), (bits[axis], keep1)):
                index = at_bits({axis: value}, 3)
                mine = parts[mat][index + (bits[3], slice(None), span)].astype(jnp.float32)
                store[mat][:, :, :, span] = mine + recv0[mat][(slot,) + index + (slice(None), span)].astype(jnp.float32)
            axis_copy(1, mat, color, block).start()

    @pl.when(step < n_steps)
    def _():
        part2[...] = dot_tn(act_buf[...], g_buf[...]).astype(jnp.bfloat16).reshape(part2.shape)
        core_copy(1, step).start()
        part1[...] = dot_tn(x_buf[...], dh_buf[...]).astype(jnp.bfloat16).reshape(part1.shape)
        core_copy(0, step).start()

    @pl.when(step < n_chunks)
    def _():
        def tile_body(tile, carry):
            rows = pl.ds(pl.multiple_of(tile * TILE, TILE), TILE)
            acc[rows, :] += dot_nt(dh_buf[rows, :], w1_ref[...])
            return carry
        lax.fori_loop(0, tokens // TILE, tile_body, 0)

    @pl.when(step == n_chunks - 1)
    def _():
        def tile_body(tile, carry):
            rows = pl.ds(pl.multiple_of(tile * TILE, TILE), TILE)
            g_buf[rows, :] = (g_buf[rows, :].astype(jnp.float32) + acc[rows, :]).astype(jnp.bfloat16)
            return carry
        lax.fori_loop(0, tokens // TILE, tile_body, 0)


def backward_sums(x_tokens, grad_tokens, w_up, w_down, n_dev):
    layers, model_width, ff_width = w_up.shape
    tokens = grad_tokens.shape[0]
    chunk = 512
    n_chunks = ff_width // chunk
    per_dev = chunk // n_dev
    rows_up = model_width // n_dev
    n_steps = layers * n_chunks
    cols = (((0, chunk // 4), (chunk // 4, chunk // 2), (chunk // 2, chunk)), ((0, 384), (384, 768), (768, model_width)))
    w1_view = w_up.reshape(layers, model_width, n_dev, n_chunks, per_dev).transpose(0, 3, 1, 2, 4).reshape(layers, n_chunks, model_width, chunk)
    w2_view = w_down.reshape(layers, n_dev, n_chunks, per_dev, model_width)

    def where(step):
        last = jnp.minimum(step, n_steps - 1)
        return layers - 1 - last // n_chunks, lax.rem(last, n_chunks)

    def pair(lead, dtype):
        return [pltpu.VMEM(lead + (rows_up, chunk), dtype), pltpu.VMEM(lead + (per_dev, model_width), dtype)]

    f32, b16 = jnp.float32, jnp.bfloat16
    scratch = [pltpu.VMEM((tokens, model_width), b16), pltpu.VMEM((tokens, model_width), b16), pltpu.VMEM((tokens, model_width), f32),
               pltpu.VMEM((tokens, chunk), b16), pltpu.VMEM((tokens, chunk), b16)]
    scratch += pair((2, 2, 2, 2), b16) + pair((2, 2, 2, 2), b16)
    for lead in ((2, 2), (2,), ()):
        scratch += pair(lead, f32) + pair(lead, f32) + pair((2,) + lead, f32)
    dma = pltpu.SemaphoreType.DMA
    scratch += [dma((2,)), dma((2,)), dma((2, 2)), dma((18,)), dma((18, 2))]
    hbm = pl.BlockSpec(memory_space=pl.ANY)
    out1, out2 = pl.pallas_call(
        functools.partial(backward_kernel, n_steps, n_chunks, cols),
        grid=(n_steps + 4,),
        in_specs=[hbm, hbm,
                  pl.BlockSpec((None, None, model_width, chunk), lambda s: (*where(s), 0, 0)),
                  pl.BlockSpec((None, n_dev, None, per_dev, model_width), lambda s: (where(s)[0], 0, where(s)[1], 0, 0))],
        out_specs=[pl.BlockSpec((None, rows_up, chunk), lambda s: (jnp.maximum(s - 4, 0), 0, 0)),
                   pl.BlockSpec((None, per_dev, model_width), lambda s: (jnp.maximum(s - 4, 0), 0, 0))],
        out_shape=[jax.ShapeDtypeStruct((n_steps, rows_up, chunk), f32), jax.ShapeDtypeStruct((n_steps, per_dev, model_width), f32)],
        scratch_shapes=scratch,
        compiler_params=pltpu.CompilerParams(vmem_limit_bytes=67_043_328, dimension_semantics=("arbitrary",), collective_id=0, has_side_effects=True),
        cost_estimate=pl.CostEstimate(flops=18 * tokens * model_width * ff_width, bytes_accessed=60_000_000, transcendentals=2 * tokens * ff_width),
        name="backward_reduce",
    )(x_tokens, grad_tokens, w1_view, w2_view)
    sums_up = out1.reshape(layers, n_chunks, rows_up, n_dev, per_dev)[::-1].transpose(0, 2, 3, 1, 4).reshape(layers, rows_up, ff_width)
    sums_down = out2.reshape(layers, n_chunks * per_dev, model_width)[::-1]
    return sums_up, sums_down


def solution(mesh):
    n_dev = mesh.shape["fsdp"]
    rows_spec = P(None, "fsdp")

    def local_step(x_saved, grad_out, x_next, w_up, w_down, gacc_up, gacc_down, master_up, master_down, mom1_up, mom1_down, mom2_up, mom2_down):
        layers, model_width, ff_width = w_up.shape
        clip_norm = 0.1 * math.sqrt(2 * layers * model_width * ff_width)
        sums_up, sums_down = backward_sums(x_saved.reshape(layers, -1, model_width), grad_out.reshape(-1, model_width), w_up, w_down, n_dev)
        grad_up = (gacc_up + sums_up) / MICRO_STEPS
        grad_down = (gacc_down + sums_down) / MICRO_STEPS
        local_sq = jnp.sum(grad_up * grad_up) + jnp.sum(grad_down * grad_down)
        clip_factor = jnp.minimum(1.0, clip_norm / jnp.sqrt(lax.psum(local_sq, "fsdp")))
        new_up = adamw_update(master_up, mom1_up, mom2_up, grad_up * clip_factor)
        new_down = adamw_update(master_down, mom1_down, mom2_down, grad_down * clip_factor)
        up_shard = new_up[0].astype(jnp.bfloat16)
        down_shard = new_down[0].astype(jnp.bfloat16)
        hidden_state = x_next.reshape(-1, x_next.shape[2])
        for layer_idx in range(layers):
            w_layer_up = lax.all_gather(up_shard[layer_idx], "fsdp", axis=0, tiled=True)
            w_layer_down = lax.all_gather(down_shard[layer_idx], "fsdp", axis=0, tiled=True)
            pre_act = jnp.dot(hidden_state, w_layer_up, preferred_element_type=jnp.float32)
            hidden_act = gelu_fn(pre_act).astype(jnp.bfloat16)
            hidden_state = (hidden_state.astype(jnp.float32) + jnp.dot(hidden_act, w_layer_down, preferred_element_type=jnp.float32)).astype(jnp.bfloat16)
        return (hidden_state.reshape(x_next.shape), new_up[0], new_down[0], new_up[1], new_down[1], new_up[2], new_down[2])

    return jax.shard_map(local_step, mesh=mesh, in_specs=(rows_spec, P("fsdp"), P("fsdp"), P(), P(), rows_spec, rows_spec, rows_spec, rows_spec, rows_spec, rows_spec, rows_spec, rows_spec), out_specs=(P("fsdp"), rows_spec, rows_spec, rows_spec, rows_spec, rows_spec, rows_spec), check_vma=False)
```

time: 861 us -> 744 us (0.86)
  matrix products: 524 us -> 158 us
  Pallas kernels: 0 us -> 362 us
  waiting for transfers between devices: 211 us -> 68.1 us
  local copies, waits for them, and re-layouts: 11.7 us -> 86.5 us
  other arithmetic: 39.2 us -> 19.1 us
  starting transfers between devices: 19.1 us -> 0.16 us
    dot_general x9 -> x0, matrix products: 375 us -> none  [the longest x2 128 us: backward_update(): lax.dot_general(grad_cur, w_down[layer_idx], (((1,), (1,)), ((), ())), pr...]
    pallas_call x0 -> x1, Pallas kernels: none -> 362 us  [backward_sums(): pl.pallas_call(functools.partial(backward_kernel, n_steps, n_chunks, cols...]
    all_to_all x4 -> x0, waiting for transfers between devices: 132 us -> none  [reduce_rows(): received = lax.all_to_all(part_grad, 'fsdp', 0, 0, tiled=True)]
    reshape x0 -> x2, local copies, waits for them, and re-layouts: none -> 38.7 us  [the longest x1 21.6 us: backward_sums(): w_up.reshape(layers, model_width, n_dev, n_chunks, per_dev)]
    unnamed x24 -> x7, local copies, waits for them, and re-layouts: 1.02 us -> 22.1 us
    transpose x0 -> x3, local copies, waits for them, and re-layouts: none -> 19.7 us  [the longest x1 14.2 us: backward_sums(): w_up.reshape(layers, model_width, n_dev, n_chunks, per_dev)]
    reduce_sum x6 -> x2, other arithmetic: 23.7 us -> 4.75 us  [local_step(): local_sq = jnp.sum(grad_up * grad_up) + jnp.sum(grad_down * grad_down)]
    all_to_all x4 -> x0, starting transfers between devices: 18.3 us -> none  [reduce_rows(): received = lax.all_to_all(part_grad, 'fsdp', 0, 0, tiled=True)]
  transfers between devices with their start and end apart: 8 -> 4, of which waited for: 7 -> 4; matrix products, arithmetic and copies ran while one was open for 52% -> 18% of each run, Pallas kernels for 0% -> 0%
where the time goes in v1:
time: 744 us; the launch traced here: 741 us
  Pallas kernels  362 us (49%)
  matrix products  158 us (21%)
  local copies, waits for them, and re-layouts  86.5 us (12%)
  waiting for transfers between devices  68.1 us (9%)
  blocking collectives  32 us (4%)
  other arithmetic  19.1 us (3%)
  between operations  16.2 us (2%)
    pallas_call x1, Pallas kernels, backward_sums(): pl.pallas_call(functools.partial(backward_kernel, n_steps, n_chunks, cols...  362 us
    dot_general x2, matrix products, local_step(): jnp.dot(hidden_state, w_layer_up, preferred_element_type=jnp.float32)  91.3 us
    dot_general x2, matrix products, local_step(): jnp.dot(hidden_act, w_layer_down, preferred_element_type=jnp.float32)  66.4 us
    all_gather x2, waiting for transfers between devices, local_step(): w_layer_up = lax.all_gather(up_shard[layer_idx], 'fsdp', axis=0, tiled=True)  56.5 us
    psum x1, blocking collectives, local_step(): lax.psum(local_sq, 'fsdp')  32 us
    unnamed x7, local copies, waits for them, and re-layouts  22.1 us
    reshape x1, local copies, waits for them, and re-layouts, backward_sums(): w_up.reshape(layers, model_width, n_dev, n_chunks, per_dev)  21.6 us
    reshape x1, local copies, waits for them, and re-layouts, backward_sums(): out1.reshape(layers, n_chunks, rows_up, n_dev, per_dev)[::-1]  17.1 us
  transfers between devices with their start and end apart: 4, of which 4 were waited for; matrix products, arithmetic and copies ran while one was open for 18% of the time, Pallas kernels for 0%

profile of v1, /device:TPU:0, one launch (start us, length us, event | category | flops | bytes accessed | tf_op | source)
XLA Modules:
  0.0 741.4 jit_solution(258842799216650046)
XLA Ops:
  7.2 0.0 all-gather.9.cloned.1.call-start
  7.2 21.2 %copy.65 = bf16[2,1024,4096]{1,2,0:T(8,128)(2,1)} copy(bf16[2,1024,4096]{2,1,0:T(8,128)(2,1)} %param.16) | data formatting | bytes 33554432 | tf_op args[3]
  28.5 14.2 %copy.66 = bf16[2,8,1024,16,32]{2,4,3,1,0:T(8,128)(2,1)} copy(bf16[2,8,1024,16,32]{2,4,1,3,0:T(8,128)(2,1)} %bitcast.37) | data formatting | bytes 33554432 | tf_op jit(solution)/shard_map/transpose | solution.py:207
  42.6 21.6 %copy.67.w1_ref = bf16[2,8,1024,512]{3,2,1,0:T(8,128)(2,1)} copy(bf16[2,8,1024,512]{2,3,1,0:T(8,128)(2,1)} %bitcast.36) | data formatting | bytes 33554432 | tf_op jit(solution)/shard_map/reshape | solution.py:207
  64.3 361.6 %backward_reduce.1 = (f32[16,64,512]{2,1,0:T(8,128)}, f32[16,32,1024]{2,1,0:T(8,128)}) custom-call(bf16[2,3072,1024]{2,1,0:T(8,128)(2,1)} %bitcast.43, bf16[3072,1024]{1,0:T(8,128)(2,1)} %bitcast.44, bf16[2,8,1024,512]{3,2,1,0:T(8,128)(2,1)} %copy.67.w1_ref, bf16[2,16,8,32,1024]{4,3,2,1,0:T(8,128)(2,1)} %bitcast.42), custom_call_target="tpu_custom_call" | custom-call | flops 231928233984 | bytes 60000000 | tf_op jit(solution)/shard_map/backward_reduce/pallas_call | solution.py:226
  425.8 3.8 copy.68
  429.7 2.9 reverse_bitcast_fusion
  432.6 2.7 copy.69
  435.2 17.1 %copy.70 = f32[2,64,4096]{2,1,0:T(8,128)} copy(f32[2,64,4096]{1,2,0:T(8,128)} %bitcast.39) | data formatting | bytes 4194304 | tf_op jit(solution)/shard_map/reshape | solution.py:240
  452.3 0.0 copy-start
  452.4 0.0 copy-start.2
  452.4 3.5 multiply_reduce_fusion.1
  455.9 0.0 copy-done
  455.9 0.0 copy-done.2
  455.9 1.2 multiply_reduce_fusion
  458.4 32.0 %psum.7 = f32[]{:T(128)} all-reduce(f32[]{:T(128)S(6)} %add.61), channel_id=1, replica_groups=mesh['fsdp'=16] {'fsdp'}, use_global_device_ids=true, to_apply=%region_2.0 | all-reduce | flops 1 | bytes 8 | tf_op jit(solution)/shard_map/psum | solution.py:256
  491.1 6.7 fusion.30
  497.8 0.0 copy-start.1
  497.8 1.0 fusion.33
  498.8 0.0 all-gather.9.cloned.1.call-update
  498.9 0.0 all-gather.11.cloned.1.call-start
  498.9 0.9 copy-done.1
  499.8 7.6 %fusion.28 = (bf16[2,256,1024]{2,1,0:T(8,128)(2,1)S(1)}, f32[2,256,1024]{2,1,0:T(8,128)}, f32[2,256,1024]{2,1,0:T(8,128)}, f32[2,256,1024]{2,1,0:T(8,128)}) fusion(f32[2,256,1024]{2,1,0:T(8,128)} %param.21, f32[]{:T(128)S(6)} %mul.114, f32[2,256,1024]{2,1,0:T(8,128)S(1)} %copy-done.1, f32[2,256,1024]{2,1,0:T(8,128)} %bitcast.40, f32[2,256,1024]{2,1,0:T(8,128)} %param.23, ...), kind=kLoop, calls=%fused_computation.38 | loop fusion | flops 9437184 | bytes 17825796 | tf_op jit(solution)/shard_map/convert_element_type | solution.py:260
  507.4 1.1 fusion.32
  508.5 0.0 all-gather.11.cloned.1.call-update
  508.5 0.0 all-gather.13.cloned.1.call-start
  508.6 0.7 all-gather.13.cloned.1.call-update
  509.2 0.0 all-gather.15.cloned.1.call-start
  509.3 0.5 all-gather.15.cloned.1.call-update
  509.8 38.7 %all-gather.9.cloned.1.call-done = bf16[1,1024,4096]{2,1,0:T(8,128)(2,1)} async-done(((bf16[1,64,4096]{2,1,0:T(8,128)(2,1)}), bf16[1,1024,4096]{2,1,0:T(8,128)(2,1)}) %all-gather.9.cloned.1.call-update) | async-done | bytes 8388624 | tf_op jit(solution)/shard_map/all_gather | solution.py:263
  548.5 46.9 %fusion.7 = bf16[3072,4096]{0,1:T(8,128)(2,1)} fusion(bf16[3072,1024]{1,0:T(8,128)(2,1)} %bitcast.45, bf16[1,1024,4096]{2,1,0:T(8,128)(2,1)} %all-gather.9.cloned.1.call-done), kind=kOutput, calls=%fused_computation.9 | convolution fusion | flops 25883049984 | bytes 39845888 | tf_op jit(solution)/shard_map/dot_general | solution.py:265
  595.4 4.1 all-gather.11.cloned.1.call-done
  599.4 33.1 %add_convert_fusion.1 = bf16[3072,1024]{1,0:T(8,128)(2,1)} fusion(bf16[3072,1024]{1,0:T(8,128)(2,1)} %bitcast.46, bf16[3072,4096]{0,1:T(8,128)(2,1)} %fusion.7, bf16[1,4096,1024]{2,1,0:T(8,128)(2,1)} %all-gather.11.cloned.1.call-done), kind=kOutput, calls=%fused_computation.19 | convolution fusion | flops 25779240960 | bytes 46137344 | tf_op jit(solution)/shard_map/dot_general | solution.py:267
  632.5 17.9 %all-gather.13.cloned.1.call-done = bf16[1,1024,4096]{2,1,0:T(8,128)(2,1)} async-done(((bf16[1,64,4096]{2,1,0:T(8,128)(2,1)}), bf16[1,1024,4096]{2,1,0:T(8,128)(2,1)}) %all-gather.13.cloned.1.call-update) | async-done | bytes 8388624 | tf_op jit(solution)/shard_map/all_gather | solution.py:263
  650.3 44.5 %fusion.15 = bf16[3072,4096]{0,1:T(8,128)(2,1)} fusion(bf16[3072,1024]{1,0:T(8,128)(2,1)} %add_convert_fusion.1, bf16[1,1024,4096]{2,1,0:T(8,128)(2,1)} %all-gather.13.cloned.1.call-done), kind=kOutput, calls=%fused_computation.17 | convolution fusion | flops 25883049984 | bytes 39845888 | tf_op jit(solution)/shard_map/dot_general | solution.py:265
  694.8 6.3 all-gather.15.cloned.1.call-done
  701.1 33.3 %add_convert_fusion = bf16[3072,1024]{1,0:T(8,128)(2,1)} fusion(bf16[3072,1024]{1,0:T(8,128)(2,1)} %add_convert_fusion.1, bf16[3072,4096]{0,1:T(8,128)(2,1)} %fusion.15, bf16[1,4096,1024]{2,1,0:T(8,128)(2,1)} %all-gather.15.cloned.1.call-done), kind=kOutput, calls=%fused_computation.18 | convolution fusion | flops 25779240960 | bytes 46137344 | tf_op jit(solution)/shard_map/dot_general | solution.py:267
Async XLA Ops:
  7.2 541.3 %all-gather.9.cloned.1.call-start = ((), (), s32[]{:S(2)}) async-start(), calls=%async_computation | async-start | bytes 8912896 | tf_op jit(solution)/shard_map/all_gather | solution.py:263
  452.3 3.6 copy-start
  452.4 3.5 copy-start.2
  497.8 2.0 copy-start.1
  498.9 100.6 %all-gather.11.cloned.1.call-start = ((), (), s32[]{:S(2)}) async-start(), calls=%async_computation.1 | async-start | bytes 8912896 | tf_op jit(solution)/shard_map/all_gather | solution.py:264
  508.5 141.8 %all-gather.13.cloned.1.call-start = ((), (), s32[]{:S(2)}) async-start(), calls=%async_computation.2 | async-start | bytes 8912896 | tf_op jit(solution)/shard_map/all_gather | solution.py:263
  509.2 191.9 %all-gather.15.cloned.1.call-start = ((), (), s32[]{:S(2)}) async-start(), calls=%async_computation.3 | async-start | bytes 8912896 | tf_op jit(solution)/shard_map/all_gather | solution.py:264
Sparse Core Ops, SparseCore 0:
  499.0 49.4 all-gather.8
  550.7 48.6 all-gather.10
  601.7 48.6 all-gather.12
  652.4 48.6 all-gather.14

commit v2 on v1

--- a/solution.py
+++ b/solution.py
@@ -21,10 +21,8 @@
 STRIDES = (8, 4, 2, 1)
 ORDERS = ((2, 1, 0), (1, 0, 2), (0, 2, 1))
 TILE = 512
-
-
-def gelu_fn(pre_act):
-    return jax.nn.gelu(pre_act, approximate=True)
+LANES = 128
+ROWS = 128
 
 
 def adamw_update(master_old, mom_one, mom_two, grad_clip):
@@ -48,11 +46,10 @@
     return tuple(picks.get(dim, slice(None)) for dim in range(count))
 
 
-def backward_kernel(n_steps, n_chunks, cols, x_hbm, g_hbm, w1_ref, w2_ref, out1_ref, out2_ref, x_buf, g_buf, acc, act_buf, dh_buf, part1, part2, *rest):
+def backward_kernel(n_steps, n_chunks, cols, x_hbm, g_hbm, w1_hbm, w2_ref, out1_ref, out2_ref, x_buf, g_buf, acc, act_buf, dh_buf, w1_group, w1_ref, part1, part2, *rest):
     parts = (part1, part2)
     recv0, send1, keep1, recv1, send2, keep2, recv2, send3, keep3, recv3 = (rest[2 * i:2 * i + 2] for i in range(10))
-    load_sem, send_sem0, recv_sem0, send_sem, recv_sem = rest[20:]
-    outs = (out1_ref, out2_ref)
+    load_sem, group_sem, send_sem0, recv_sem0, send_sem, recv_sem = rest[20:]
     step = pl.program_id(0)
     me = lax.axis_index("fsdp")
     bits = [lax.rem(me // stride, 2) for stride in STRIDES]
@@ -82,8 +79,21 @@
             for color in range(3):
                 yield mat, color, pl.ds(cols[mat][color][0], cols[mat][color][1] - cols[mat][color][0])
 
+    n_dev, per_dev = w2_ref.shape[:2]
+    spread = LANES // per_dev
+
+    def lane_part():
+        return lax.broadcasted_iota(jnp.int32, (ROWS, LANES), 1) // per_dev
+
+    def group_copies(layer, half):
+        return [pltpu.make_async_copy(
+            w1_hbm.at[layer, :, pl.ds(pl.multiple_of((dev * n_chunks // spread + half) * LANES, LANES), LANES)],
+            w1_group.at[dev], group_sem.at[dev]) for dev in range(n_dev)]
+
     @pl.when(step == 0)
     def _():
+        for copy in group_copies(w1_hbm.shape[0] - 1, 0):
+            copy.start()
         barrier = pltpu.get_barrier_semaphore()
         for peer in peers:
             pl.semaphore_signal(barrier, inc=1, device_id=(peer,), device_id_type=MESH)
@@ -101,6 +111,34 @@
         load_x = pltpu.make_async_copy(x_hbm.at[0], x_buf, load_sem.at[0])
         load_x.start()
         load_x.wait()
+
+    @pl.when((step < n_steps) & (lax.rem(step, spread) == 0))
+    def _():
+        for copy in group_copies(0, 0):
+            copy.wait()
+
+    @pl.when(step < n_steps)
+    def _():
+        phase = lax.rem(step, spread)
+
+        def row_body(block, carry):
+            rows = pl.ds(pl.multiple_of(block * ROWS, ROWS), ROWS)
+            part = lane_part()
+            for tile in range(n_dev // spread):
+                merged = None
+                for place in range(spread):
+                    moved = w1_group[tile * spread + place, rows, :].astype(jnp.float32)
+                    moved = pltpu.roll(moved, lax.rem(place - phase + spread, spread) * per_dev, 1)
+                    merged = moved if merged is None else jnp.where(part == place, moved, merged)
+                w1_ref[rows, tile * LANES:(tile + 1) * LANES] = merged.astype(jnp.bfloat16)
+            return carry
+        lax.fori_loop(0, w1_ref.shape[0] // ROWS, row_body, 0)
+
+    @pl.when((step < n_steps - 1) & (lax.rem(step, spread) == spread - 1))
+    def _():
+        following = step + 1
+        for copy in group_copies(w1_hbm.shape[0] - 1 - following // n_chunks, lax.rem(following, n_chunks) // spread):
+            copy.start()
 
     @pl.when(step < n_steps)
     def _():
@@ -124,7 +162,23 @@
             copy = axis_copy(3, mat, color, block)
             copy.wait_send()
             copy.wait_recv()
-            outs[mat][:, span] = keep3[mat][:, span] + recv3[mat][lax.rem(block, 2), :, span]
+            total = keep3[mat][:, span] + recv3[mat][lax.rem(block, 2), :, span]
+            if mat == 1:
+                out2_ref[:, span] = total
+            else:
+                keep3[0][:, span] = total
+        chunk = lax.rem(block, n_chunks)
+
+        @pl.when(chunk == 0)
+        def _():
+            out1_ref[...] = jnp.zeros_like(out1_ref)
+        phase = lax.rem(chunk, spread)
+        part = lax.broadcasted_iota(jnp.int32, (out1_ref.shape[0], LANES), 1) // per_dev
+        for dev in range(n_dev):
+            tile = dev // spread
+            moved = pltpu.roll(keep3[0][:, tile * LANES:(tile + 1) * LANES], lax.rem(phase - dev % spread + spread, spread) * per_dev, 1)
+            spot = pl.ds(pl.multiple_of((dev * n_chunks // spread + chunk // spread) * LANES, LANES), LANES)
+            out1_ref[:, spot] = jnp.where(part == phase, moved, out1_ref[:, spot])
 
     @pl.when((step >= 3) & (step < n_steps + 3))
     def _():
@@ -204,7 +258,6 @@
     rows_up = model_width // n_dev
     n_steps = layers * n_chunks
     cols = (((0, chunk // 4), (chunk // 4, chunk // 2), (chunk // 2, chunk)), ((0, 384), (384, 768), (768, model_width)))
-    w1_view = w_up.reshape(layers, model_width, n_dev, n_chunks, per_dev).transpose(0, 3, 1, 2, 4).reshape(layers, n_chunks, model_width, chunk)
     w2_view = w_down.reshape(layers, n_dev, n_chunks, per_dev, model_width)
 
     def where(step):
@@ -216,30 +269,251 @@
 
     f32, b16 = jnp.float32, jnp.bfloat16
     scratch = [pltpu.VMEM((tokens, model_width), b16), pltpu.VMEM((tokens, model_width), b16), pltpu.VMEM((tokens, model_width), f32),
-               pltpu.VMEM((tokens, chunk), b16), pltpu.VMEM((tokens, chunk), b16)]
+               pltpu.VMEM((tokens, chunk), b16), pltpu.VMEM((tokens, chunk), b16),
+               pltpu.VMEM((n_dev, model_width, LANES), b16), pltpu.VMEM((model_width, chunk), b16)]
     scratch += pair((2, 2, 2, 2), b16) + pair((2, 2, 2, 2), b16)
     for lead in ((2, 2), (2,), ()):
         scratch += pair(lead, f32) + pair(lead, f32) + pair((2,) + lead, f32)
     dma = pltpu.SemaphoreType.DMA
-    scratch += [dma((2,)), dma((2,)), dma((2, 2)), dma((18,)), dma((18, 2))]
+    scratch += [dma((2,)), dma((n_dev,)), dma((2,)), dma((2, 2)), dma((18,)), dma((18, 2))]
     hbm = pl.BlockSpec(memory_space=pl.ANY)
     out1, out2 = pl.pallas_call(
         functools.partial(backward_kernel, n_steps, n_chunks, cols),
         grid=(n_steps + 4,),
         in_specs=[hbm, hbm,
-                  pl.BlockSpec((None, None, model_width, chunk), lambda s: (*where(s), 0, 0)),
+                  hbm,
                   pl.BlockSpec((None, n_dev, None, per_dev, model_width), lambda s: (where(s)[0], 0, where(s)[1], 0, 0))],
-        out_specs=[pl.BlockSpec((None, rows_up, chunk), lambda s: (jnp.maximum(s - 4, 0), 0, 0)),
-                   pl.BlockSpec((None, per_dev, model_width), lambda s: (jnp.maximum(s - 4, 0), 0, 0))],
-        out_shape=[jax.ShapeDtypeStruct((n_steps, rows_up, chunk), f32), jax.ShapeDtypeStruct((n_steps, per_dev, model_width), f32)],
+        out_specs=[pl.BlockSpec((None, rows_up, ff_width), lambda s: (where(jnp.maximum(s - 4, 0))[0], 0, 0)),
+                   pl.BlockSpec((None, per_dev, model_width), lambda s: (*where(jnp.maximum(s - 4, 0)), 0))],
+        out_shape=[jax.ShapeDtypeStruct((layers, rows_up, ff_width), f32), jax.ShapeDtypeStruct((layers, n_chunks * per_dev, model_width), f32)],
         scratch_shapes=scratch,
         compiler_params=pltpu.CompilerParams(vmem_limit_bytes=67_043_328, dimension_semantics=("arbitrary",), collective_id=0, has_side_effects=True),
         cost_estimate=pl.CostEstimate(flops=18 * tokens * model_width * ff_width, bytes_accessed=60_000_000, transcendentals=2 * tokens * ff_width),
         name="backward_reduce",
-    )(x_tokens, grad_tokens, w1_view, w2_view)
-    sums_up = out1.reshape(layers, n_chunks, rows_up, n_dev, per_dev)[::-1].transpose(0, 2, 3, 1, 4).reshape(layers, rows_up, ff_width)
-    sums_down = out2.reshape(layers, n_chunks * per_dev, model_width)[::-1]
-    return sums_up, sums_down
+    )(x_tokens, grad_tokens, w_up, w2_view)
+    return out1, out2
+
+
+def norm_kernel(n_dev, value_ref, out_ref, gathered, send_sem, recv_sem):
+    me = lax.axis_index("fsdp")
+    barrier = pltpu.get_barrier_semaphore()
+    for shift in range(1, n_dev):
+        pl.semaphore_signal(barrier, inc=1, device_id=(lax.rem(me + shift, n_dev),), device_id_type=MESH)
+    pl.semaphore_wait(barrier, n_dev - 1)
+
+    def copy_of(shift, sender):
+        return pltpu.make_async_remote_copy(
+            src_ref=value_ref, dst_ref=gathered.at[sender], send_sem=send_sem.at[shift], recv_sem=recv_sem.at[sender],
+            device_id=(lax.rem(me + shift, n_dev),), device_id_type=MESH)
+
+    for shift in range(1, n_dev):
+        copy_of(shift, me).start()
+    gathered[me] = value_ref[...]
+    for shift in range(1, n_dev):
+        copy_of(shift, lax.rem(me + n_dev - shift, n_dev)).wait_recv()
+    total = gathered[0]
+    for dev in range(1, n_dev):
+        total = total + gathered[dev]
+    out_ref[...] = total
+    for shift in range(1, n_dev):
+        copy_of(shift, me).wait_send()
+
+
+def global_sum(value, n_dev):
+    tile = jnp.broadcast_to(value, (8, LANES))
+    vmem = pl.BlockSpec(memory_space=pltpu.VMEM)
+    dma = pltpu.SemaphoreType.DMA
+    return pl.pallas_call(
+        functools.partial(norm_kernel, n_dev), in_specs=[vmem], out_specs=vmem,
+        out_shape=jax.ShapeDtypeStruct(tile.shape, jnp.float32),
+        scratch_shapes=[pltpu.VMEM((n_dev,) + tile.shape, jnp.float32), dma((n_dev,)), dma((n_dev,))],
+        compiler_params=pltpu.CompilerParams(collective_id=1, has_side_effects=True),
+        name="norm_sum")(tile)[0, 0]
+
+
+def forward_kernel(x_hbm, up0_hbm, down0_hbm, up1_hbm, down1_hbm, y_hbm, h_buf, act_buf, buf_a, buf_b, buf_c, load_sem, free_sem, send_sem, recv_sem):
+    shards = (up0_hbm, down0_hbm, up1_hbm, down1_hbm)
+    bufs = (buf_a, buf_b, buf_c, buf_a)
+    me = lax.axis_index("fsdp")
+    bits = [lax.rem(me // stride, 2) for stride in STRIDES]
+    peers = [me + (1 - 2 * bit) * stride for bit, stride in zip(bits, STRIDES)]
+    rows = up0_hbm.shape[0]
+    tokens, width = h_buf.shape
+    quarter = rows // 4
+    pieces = ((0, 0, rows // 2), (0, rows // 2, rows), (1, 0, rows), (2, 0, rows), (3, 0, rows))
+    n_tiles = tokens // TILE
+
+    def spans(piece):
+        _, lo, hi = pieces[piece]
+        size = (hi - lo) // 16
+        third = size // 3
+        cuts = [0, third, 2 * third, size]
+        if piece % 3 == 1:
+            cuts = [0, third, size - third, size]
+        if piece % 3 == 2:
+            cuts = [0, size - 2 * third, size - third, size]
+        return [(lo + 16 * cuts[color], 16 * (cuts[color + 1] - cuts[color])) for color in range(3)]
+
+    def copies(piece, phase):
+        matrix = pieces[piece][0]
+        out = []
+        for color, (lo, size) in enumerate(spans(piece)):
+            order = ORDERS[color]
+            picks = {axis: bits[axis] for axis in range(4)}
+            for axis in order[:min(phase, 2)]:
+                picks.pop(axis)
+            if phase == 4:
+                picks[order[2]] = 1 - bits[order[2]]
+            where = at_bits(picks, 4) + (pl.ds(lo, size),)
+            axis = order[phase] if phase < 3 else 3
+            slot = (piece * 5 + phase) * 3 + color
+            out.append(pltpu.make_async_remote_copy(
+                src_ref=bufs[matrix].at[where], dst_ref=bufs[matrix].at[where],
+                send_sem=send_sem.at[slot], recv_sem=recv_sem.at[slot],
+                device_id=(peers[axis],), device_id_type=MESH))
+        return out
+
+    def start(piece, phase):
+        for copy in copies(piece, phase):
+            copy.start()
+
+    def arrived(piece, phase):
+        for copy in copies(piece, phase):
+            copy.wait_recv()
+
+    def second(piece):
+        arrived(piece, 0)
+        start(piece, 1)
+
+    def third(piece):
+        arrived(piece, 1)
+        start(piece, 2)
+        start(piece, 3)
+
+    def hand_over(piece):
+        arrived(piece, 2)
+        start(piece, 4)
+
+    def complete(piece):
+        arrived(piece, 3)
+        arrived(piece, 4)
+
+    def load(matrix):
+        return pltpu.make_async_copy(shards[matrix], bufs[matrix].at[tuple(bits)], load_sem.at[matrix])
+
+    barrier = pltpu.get_barrier_semaphore()
+    for peer in peers:
+        pl.semaphore_signal(barrier, inc=1, device_id=(peer,), device_id_type=MESH)
+    for matrix in range(3):
+        load(matrix).start()
+    load_x = pltpu.make_async_copy(x_hbm, h_buf, load_sem.at[4])
+    load_x.start()
+    load(0).wait()
+    pl.semaphore_wait(barrier, 4)
+    start(0, 0)
+    start(1, 0)
+    load(1).wait()
+    load(2).wait()
+    second(0)
+    second(1)
+    third(0)
+    start(2, 0)
+    hand_over(0)
+    third(1)
+    second(2)
+    start(3, 0)
+    load_x.wait()
+    complete(0)
+
+    def weights(matrix, block):
+        return bufs[matrix][:, :, :, :, pl.ds(pl.multiple_of(block * quarter, quarter), quarter), :].reshape(4 * 4 * quarter, width)
+
+    def run(count, matrix, body, events):
+        def step(index, carry):
+            for when, event in events.items():
+                pl.when(index == when)(event)
+            body(index, matrix)
+            return carry
+        lax.fori_loop(0, count, step, 0)
+
+    def up(index, matrix):
+        block, tile = index // n_tiles, lax.rem(index, n_tiles)
+        span = pl.ds(pl.multiple_of(tile * TILE, TILE), TILE)
+        pre = jnp.dot(h_buf[span, :], weights(matrix, block), preferred_element_type=jnp.float32)
+        gate = 0.5 + 0.5 * jnp.tanh(pre * (GELU_A + GELU_B * (pre * pre)))
+        act_buf[block, span, :] = (pre * gate).astype(jnp.bfloat16)
+
+    def down(tile, matrix):
+        span = pl.ds(pl.multiple_of(tile * TILE, TILE), TILE)
+        total = h_buf[span, :].astype(jnp.float32)
+        for block in range(4):
+            total = total + jnp.dot(act_buf[block, span, :], bufs[matrix][block // 2, block % 2].reshape(width, width), preferred_element_type=jnp.float32)
+        h_buf[span, :] = total.astype(jnp.bfloat16)
+
+    def store(tile):
+        span = pl.ds(pl.multiple_of(tile * TILE, TILE), TILE)
+        return pltpu.make_async_copy(h_buf.at[span, :], y_hbm.at[span, :], load_sem.at[5 + tile])
+
+    def down_last(tile, matrix):
+        down(tile, matrix)
+        store(tile).start()
+
+    def event_second():
+        hand_over(1)
+        third(2)
+        second(3)
+
+    def event_third():
+        hand_over(2)
+        third(3)
+
+    def event_fourth():
+        hand_over(3)
+        third(4)
+
+    run(4 * n_tiles, 0, up, {2 * n_tiles - 1: event_second, 2 * n_tiles: lambda: complete(1), 4 * n_tiles - 1: event_third})
+    for piece in (0, 1):
+        for phase in range(5):
+            for copy in copies(piece, phase):
+                copy.wait_send()
+    for peer in peers:
+        pl.semaphore_signal(free_sem, inc=1, device_id=(peer,), device_id_type=MESH)
+    load(3).start()
+    complete(2)
+    load(3).wait()
+    pl.semaphore_wait(free_sem, 4)
+    start(4, 0)
+    run(n_tiles, 1, down, {2: lambda: second(4), n_tiles - 1: event_fourth})
+    complete(3)
+    run(4 * n_tiles, 2, up, {4 * n_tiles - 3: lambda: hand_over(4)})
+    complete(4)
+    run(n_tiles, 3, down_last, {})
+    for piece in (2, 3, 4):
+        for phase in range(5):
+            for copy in copies(piece, phase):
+                copy.wait_send()
+    for tile in range(n_tiles):
+        store(tile).wait()
+
+
+def forward_stack(x_tokens, up_shard, down_shard, n_dev):
+    tokens, model_width = x_tokens.shape
+    layers, rows, ff_width = up_shard.shape
+    blocks = ff_width // model_width
+    up_blocks = up_shard.reshape(layers, rows, blocks, model_width).transpose(0, 2, 1, 3).reshape(layers, blocks * rows, model_width)
+    hbm = pl.BlockSpec(memory_space=pl.ANY)
+    b16 = jnp.bfloat16
+    gathered = pltpu.VMEM((2, 2, 2, 2, blocks * rows, model_width), b16)
+    dma = pltpu.SemaphoreType.DMA
+    return pl.pallas_call(
+        forward_kernel, in_specs=[hbm] * 5, out_specs=hbm,
+        out_shape=jax.ShapeDtypeStruct((tokens, model_width), b16),
+        scratch_shapes=[pltpu.VMEM((tokens, model_width), b16), pltpu.VMEM((blocks, tokens, model_width), b16), gathered, gathered, gathered,
+                        dma((5 + tokens // TILE,)), pltpu.SemaphoreType.REGULAR, dma((75,)), dma((75,))],
+        compiler_params=pltpu.CompilerParams(vmem_limit_bytes=67_043_328, collective_id=2, has_side_effects=True),
+        cost_estimate=pl.CostEstimate(flops=8 * tokens * model_width * ff_width, bytes_accessed=20_000_000, transcendentals=2 * tokens * ff_width),
+        name="gather_forward",
+    )(x_tokens, up_blocks[0], down_shard[0], up_blocks[1], down_shard[1])
 
 
 def solution(mesh):
@@ -253,18 +527,12 @@
         grad_up = (gacc_up + sums_up) / MICRO_STEPS
         grad_down = (gacc_down + sums_down) / MICRO_STEPS
         local_sq = jnp.sum(grad_up * grad_up) + jnp.sum(grad_down * grad_down)
-        clip_factor = jnp.minimum(1.0, clip_norm / jnp.sqrt(lax.psum(local_sq, "fsdp")))
+        clip_factor = jnp.minimum(1.0, clip_norm / jnp.sqrt(global_sum(local_sq, n_dev)))
         new_up = adamw_update(master_up, mom1_up, mom2_up, grad_up * clip_factor)
         new_down = adamw_update(master_down, mom1_down, mom2_down, grad_down * clip_factor)
         up_shard = new_up[0].astype(jnp.bfloat16)
         down_shard = new_down[0].astype(jnp.bfloat16)
-        hidden_state = x_next.reshape(-1, x_next.shape[2])
-        for layer_idx in range(layers):
-            w_layer_up = lax.all_gather(up_shard[layer_idx], "fsdp", axis=0, tiled=True)
-            w_layer_down = lax.all_gather(down_shard[layer_idx], "fsdp", axis=0, tiled=True)
-            pre_act = jnp.dot(hidden_state, w_layer_up, preferred_element_type=jnp.float32)
-            hidden_act = gelu_fn(pre_act).astype(jnp.bfloat16)
-            hidden_state = (hidden_state.astype(jnp.float32) + jnp.dot(hidden_act, w_layer_down, preferred_element_type=jnp.float32)).astype(jnp.bfloat16)
+        hidden_state = forward_stack(x_next.reshape(-1, model_width), up_shard, down_shard, n_dev)
         return (hidden_state.reshape(x_next.shape), new_up[0], new_down[0], new_up[1], new_down[1], new_up[2], new_down[2])
 
     return jax.shard_map(local_step, mesh=mesh, in_specs=(rows_spec, P("fsdp"), P("fsdp"), P(), P(), rows_spec, rows_spec, rows_spec, rows_spec, rows_spec, rows_spec, rows_spec, rows_spec), out_specs=(P("fsdp"), rows_spec, rows_spec, rows_spec, rows_spec, rows_spec, rows_spec), check_vma=False)

time: 744 us -> 610 us (0.82)
  Pallas kernels: 362 us -> 578 us
  matrix products: 158 us -> 0 us
  local copies, waits for them, and re-layouts: 86.5 us -> 11.2 us
  waiting for transfers between devices: 68.1 us -> 0 us
  blocking collectives: 32 us -> 0 us
  between operations: 16.2 us -> 2.7 us
    pallas_call x0 -> x2, Pallas kernels: none -> 185 us  [the longest x1 178 us: forward_stack(): pl.pallas_call(forward_kernel, in_specs=[hbm] * 5, out_specs=hbm, out_sha...]
    dot_general x4 -> x0, matrix products: 158 us -> none  [the longest x2 91.3 us: local_step(): jnp.dot(hidden_state, w_layer_up, preferred_element_type=jnp.float32)]
    all_gather x4 -> x0, waiting for transfers between devices: 66.9 us -> none  [the longest x2 56.5 us: local_step(): w_layer_up = lax.all_gather(up_shard[layer_idx], 'fsdp', axis=0, tiled=True)]
    reshape x2 -> x1, local copies, waits for them, and re-layouts: 38.7 us -> 0.08 us  [forward_stack(): up_shard.reshape(layers, rows, blocks, model_width).transpose(0, 2, 1, 3)]
    psum x1 -> x0, blocking collectives: 32 us -> none  [local_step(): lax.psum(local_sq, 'fsdp')]
    pallas_call x1, Pallas kernels: 362 us -> 393 us  [backward_sums(): pl.pallas_call(functools.partial(backward_kernel, n_steps, n_chunks, cols...]
    transpose x3 -> x0, local copies, waits for them, and re-layouts: 19.7 us -> none  [the longest x1 14.2 us: backward_sums(): w_up.reshape(layers, model_width, n_dev, n_chunks, per_dev)]
    unnamed x7 -> x11, local copies, waits for them, and re-layouts: 22.1 us -> 7.15 us
  transfers between devices with their start and end apart: 4 -> 0, of which waited for: 4 -> 0; matrix products, arithmetic and copies ran while one was open for 18% -> 0% of each run, Pallas kernels for 0% -> 0%
where the time goes in v2:
time: 610 us
  Pallas kernels  578 us (95%)
  other arithmetic  17.6 us (3%)
  local copies, waits for them, and re-layouts  11.2 us (2%)
    pallas_call x1, Pallas kernels, backward_sums(): pl.pallas_call(functools.partial(backward_kernel, n_steps, n_chunks, cols...  393 us
    pallas_call x1, Pallas kernels, forward_stack(): pl.pallas_call(forward_kernel, in_specs=[hbm] * 5, out_specs=hbm, out_sha...  178 us

profile of v2, /device:TPU:0, one launch (start us, length us, event | category | flops | bytes accessed | tf_op | source)
XLA Modules:
  0.0 609.8 jit_solution(1989560602990629856)
XLA Ops:
  0.6 393.1 %backward_reduce.1 = (f32[2,64,4096]{2,1,0:T(8,128)}, f32[2,256,1024]{2,1,0:T(8,128)}) custom-call(bf16[2,3072,1024]{2,1,0:T(8,128)(2,1)} %bitcast.25, bf16[3072,1024]{1,0:T(8,128)(2,1)} %bitcast.26, bf16[2,1024,4096]{2,1,0:T(8,128)(2,1)} %w1_hbm.1, bf16[2,16,8,32,1024]{4,3,2,1,0:T(8,128)(2,1)} %bitcast.24), custom_call_target="tpu_custom_call" | custom-call | flops 231928233984 | bytes 60000000 | tf_op jit(solution)/shard_map/backward_reduce/pallas_call | solution.py:280
  393.7 0.0 copy-start
  393.7 0.0 copy-start.4
  393.7 3.5 multiply_reduce_fusion.1
  397.3 0.0 copy-done
  397.3 0.0 copy-done.4
  397.3 2.4 multiply_reduce_fusion
  401.0 0.6 broadcast_in_dim.3.value_ref
  401.6 7.3 %norm_sum.1 = f32[8,128]{1,0:T(8,128)} custom-call(f32[8,128]{1,0:T(8,128)} %broadcast_in_dim.3.value_ref), custom_call_target="tpu_custom_call" | custom-call | tf_op jit(solution)/shard_map/norm_sum/pallas_call | solution.py:326
  408.9 1.2 slice.17
  410.8 0.0 copy-start.2
  410.8 0.0 copy-start.3
  410.8 7.7 %fusion.2 = (bf16[2,256,1024]{2,1,0:T(8,128)(2,1)S(1)}, f32[2,256,1024]{2,1,0:T(8,128)}, f32[2,256,1024]{2,1,0:T(8,128)}, f32[2,256,1024]{2,1,0:T(8,128)}) fusion(f32[2,256,1024]{2,1,0:T(8,128)} %param.21, f32[2,256,1024]{2,1,0:T(8,128)} %get-tuple-element.20, f32[]{:T(128)} %bitcast.4, f32[2,256,1024]{2,1,0:T(8,128)} %param.23, f32[2,256,1024]{2,1,0:T(8,128)} %param.25), kind=kLoop, calls=%fused_computation.13 | loop fusion | flops 8912896 | bytes 15728644 | tf_op jit(solution)/shard_map/convert_element_type | solution.py:534
  418.5 0.0 copy-start.1
  418.5 1.0 slice_bitcast_fusion
  419.6 0.0 copy-done.2
  419.6 0.0 copy-done.3
  419.6 0.9 copy-done.1
  420.5 3.8 fusion.4
  424.4 0.1 copy.23
  424.4 1.1 fusion.6
  425.5 178.1 %gather_forward.1 = bf16[3072,1024]{1,0:T(8,128)(2,1)} custom-call(bf16[3072,1024]{1,0:T(8,128)(2,1)} %bitcast.27, bf16[256,1024]{1,0:T(8,128)(2,1)} %bitcast.23, bf16[256,1024]{1,0:T(8,128)(2,1)} %get-tuple-element.24.down0_hbm, bf16[256,1024]{1,0:T(8,128)(2,1)} %bitcast.22, bf16[256,1024]{1,0:T(8,128)(2,1)} %get-tuple-element.23.down1_hbm), custom_call_target="tpu_custom_call" | custom-call | flops 103079215104 | bytes 20000000 | tf_op jit(solution)/shard_map/gather_forward/pallas_call | solution.py:508
  603.6 6.2 %copy.25 = bf16[2,1536,1024]{2,1,0:T(8,128)(2,1)} copy(bf16[2,1536,1024]{2,1,0:T(8,128)(2,1)} %bitcast.19) | data formatting | bytes 12582912
Async XLA Ops:
  393.7 3.6 copy-start
  393.7 3.5 copy-start.4
  410.8 8.8 %copy-start.2 = (f32[2,64,4096]{2,1,0:T(8,128)S(1)}, f32[2,64,4096]{2,1,0:T(8,128)}, u32[]{:S(2)}) copy-start(f32[2,64,4096]{2,1,0:T(8,128)} %param.22) | copy-start | bytes 6291460
  410.8 8.8 %copy-start.3 = (f32[2,64,4096]{2,1,0:T(8,128)S(1)}, f32[2,64,4096]{2,1,0:T(8,128)}, u32[]{:S(2)}) copy-start(f32[2,64,4096]{2,1,0:T(8,128)} %param.24) | copy-start | bytes 6291460
  418.5 2.0 copy-start.1

commit v3 on v2

--- a/solution.py
+++ b/solution.py
@@ -23,6 +23,7 @@
 TILE = 512
 LANES = 128
 ROWS = 128
+TILE_B = 384
 
 
 def adamw_update(master_old, mom_one, mom_two, grad_clip):
@@ -38,15 +39,11 @@
     return lax.dot_general(left, right, (((1,), (1,)), ((), ())), preferred_element_type=jnp.float32)
 
 
-def dot_tn(left, right):
-    return lax.dot_general(left, right, (((0,), (0,)), ((), ())), preferred_element_type=jnp.float32)
-
-
 def at_bits(picks, count):
     return tuple(picks.get(dim, slice(None)) for dim in range(count))
 
 
-def backward_kernel(n_steps, n_chunks, cols, x_hbm, g_hbm, w1_hbm, w2_ref, out1_ref, out2_ref, x_buf, g_buf, acc, act_buf, dh_buf, w1_group, w1_ref, part1, part2, *rest):
+def backward_kernel(n_steps, n_chunks, cols, x_hbm, g_hbm, w1_hbm, w2_ref, out1_ref, out2_ref, x_buf, g_buf, x_turned, acc, act_turned, dh_buf, w1_group, w1_slots, part1, part2, *rest):
     parts = (part1, part2)
     recv0, send1, keep1, recv1, send2, keep2, recv2, send3, keep3, recv3 = (rest[2 * i:2 * i + 2] for i in range(10))
     load_sem, group_sem, send_sem0, recv_sem0, send_sem, recv_sem = rest[20:]
@@ -112,48 +109,62 @@
         load_x.start()
         load_x.wait()
 
-    @pl.when((step < n_steps) & (lax.rem(step, spread) == 0))
+    w1_ref = w1_slots.at[lax.rem(step, 2)]
+
+    def order_columns(rows, phase, target):
+        part = lane_part()
+        for tile in range(n_dev // spread):
+            merged = None
+            for place in range(spread):
+                moved = w1_group[tile * spread + place, rows, :].astype(jnp.float32)
+                moved = pltpu.roll(moved, lax.rem(place - phase + spread, spread) * per_dev, 1)
+                merged = moved if merged is None else jnp.where(part == place, moved, merged)
+            target[rows, tile * LANES:(tile + 1) * LANES] = merged.astype(jnp.bfloat16)
+
+    @pl.when(step == 0)
     def _():
         for copy in group_copies(0, 0):
             copy.wait()
 
-    @pl.when(step < n_steps)
-    def _():
-        phase = lax.rem(step, spread)
-
         def row_body(block, carry):
-            rows = pl.ds(pl.multiple_of(block * ROWS, ROWS), ROWS)
-            part = lane_part()
-            for tile in range(n_dev // spread):
-                merged = None
-                for place in range(spread):
-                    moved = w1_group[tile * spread + place, rows, :].astype(jnp.float32)
-                    moved = pltpu.roll(moved, lax.rem(place - phase + spread, spread) * per_dev, 1)
-                    merged = moved if merged is None else jnp.where(part == place, moved, merged)
-                w1_ref[rows, tile * LANES:(tile + 1) * LANES] = merged.astype(jnp.bfloat16)
+            order_columns(pl.ds(pl.multiple_of(block * ROWS, ROWS), ROWS), 0, w1_slots.at[0])
             return carry
-        lax.fori_loop(0, w1_ref.shape[0] // ROWS, row_body, 0)
+        lax.fori_loop(0, x_buf.shape[1] // ROWS, row_body, 0)
 
     @pl.when((step < n_steps - 1) & (lax.rem(step, spread) == spread - 1))
     def _():
-        following = step + 1
+        for copy in group_copies(0, 0):
+            copy.wait()
+
+    def tile_body(tile, turn_x):
+        rows = pl.ds(pl.multiple_of(tile * TILE_B, TILE_B), TILE_B)
+        pre = jnp.dot(x_buf[rows, :], w1_ref[...], preferred_element_type=jnp.float32)
+        d_act = dot_nt(g_buf[rows, :], w2_ref[...].reshape(w1_ref.shape[1], w1_ref.shape[0]))
+        square = pre * pre
+        gate = 0.5 + 0.5 * jnp.tanh(pre * (GELU_A + GELU_B * square))
+        act = pre * gate
+        act_turned[:, rows] = act.astype(jnp.bfloat16).T
+        slope = gate + (act * (1.0 - gate)) * (2.0 * GELU_A + 6.0 * GELU_B * square)
+        dh_buf[rows, :] = (d_act * slope).astype(jnp.bfloat16)
+        order_columns(pl.ds(pl.multiple_of(tile * ROWS, ROWS), ROWS), lax.rem(step + 1, spread), w1_slots.at[lax.rem(step + 1, 2)])
+        if turn_x:
+            x_turned[:, rows] = x_buf[rows, :].T
+
+    first = lax.rem(step, n_chunks) == 0
+
+    @pl.when((step < n_steps) & first)
+    def _():
+        lax.fori_loop(0, tokens // TILE_B, lambda tile, carry: (tile_body(tile, True), carry)[1], 0)
+
+    @pl.when((step < n_steps) & (lax.rem(step, n_chunks) > 0))
+    def _():
+        lax.fori_loop(0, tokens // TILE_B, lambda tile, carry: (tile_body(tile, False), carry)[1], 0)
+
+    @pl.when((step < n_steps - 2) & (lax.rem(step, spread) == spread - 2))
+    def _():
+        following = step + 2
         for copy in group_copies(w1_hbm.shape[0] - 1 - following // n_chunks, lax.rem(following, n_chunks) // spread):
             copy.start()
-
-    @pl.when(step < n_steps)
-    def _():
-        def tile_body(tile, carry):
-            rows = pl.ds(pl.multiple_of(tile * TILE, TILE), TILE)
-            pre = jnp.dot(x_buf[rows, :], w1_ref[...], preferred_element_type=jnp.float32)
-            d_act = dot_nt(g_buf[rows, :], w2_ref[...].reshape(w1_ref.shape[1], w1_ref.shape[0]))
-            square = pre * pre
-            gate = 0.5 + 0.5 * jnp.tanh(pre * (GELU_A + GELU_B * square))
-            act = pre * gate
-            act_buf[rows, :] = act.astype(jnp.bfloat16)
-            slope = gate + (act * (1.0 - gate)) * (2.0 * GELU_A + 6.0 * GELU_B * square)
-            dh_buf[rows, :] = (d_act * slope).astype(jnp.bfloat16)
-            return carry
-        lax.fori_loop(0, tokens // TILE, tile_body, 0)
 
     @pl.when(step >= 4)
     def _():
@@ -227,9 +238,9 @@
 
     @pl.when(step < n_steps)
     def _():
-        part2[...] = dot_tn(act_buf[...], g_buf[...]).astype(jnp.bfloat16).reshape(part2.shape)
+        part2[...] = jnp.dot(act_turned[...], g_buf[...], preferred_element_type=jnp.float32).astype(jnp.bfloat16).reshape(part2.shape)
         core_copy(1, step).start()
-        part1[...] = dot_tn(x_buf[...], dh_buf[...]).astype(jnp.bfloat16).reshape(part1.shape)
+        part1[...] = jnp.dot(x_turned[...], dh_buf[...], preferred_element_type=jnp.float32).astype(jnp.bfloat16).reshape(part1.shape)
         core_copy(0, step).start()
 
     @pl.when(step < n_chunks)
@@ -268,9 +279,9 @@
         return [pltpu.VMEM(lead + (rows_up, chunk), dtype), pltpu.VMEM(lead + (per_dev, model_width), dtype)]
 
     f32, b16 = jnp.float32, jnp.bfloat16
-    scratch = [pltpu.VMEM((tokens, model_width), b16), pltpu.VMEM((tokens, model_width), b16), pltpu.VMEM((tokens, model_width), f32),
-               pltpu.VMEM((tokens, chunk), b16), pltpu.VMEM((tokens, chunk), b16),
-               pltpu.VMEM((n_dev, model_width, LANES), b16), pltpu.VMEM((model_width, chunk), b16)]
+    scratch = [pltpu.VMEM((tokens, model_width), b16), pltpu.VMEM((tokens, model_width), b16), pltpu.VMEM((model_width, tokens), b16),
+               pltpu.VMEM((tokens, model_width), f32), pltpu.VMEM((chunk, tokens), b16), pltpu.VMEM((tokens, chunk), b16),
+               pltpu.VMEM((n_dev, model_width, LANES), b16), pltpu.VMEM((2, model_width, chunk), b16)]
     scratch += pair((2, 2, 2, 2), b16) + pair((2, 2, 2, 2), b16)
     for lead in ((2, 2), (2,), ()):
         scratch += pair(lead, f32) + pair(lead, f32) + pair((2,) + lead, f32)

time: 610 us -> 589 us (0.966)
  Pallas kernels: 578 us -> 557 us
    pallas_call x1, Pallas kernels: 393 us -> 372 us  [backward_sums(): pl.pallas_call(functools.partial(backward_kernel, n_steps, n_chunks, cols...]
where the time goes in v3:
time: 589 us
  Pallas kernels  557 us (95%)
  other arithmetic  17.6 us (3%)
  local copies, waits for them, and re-layouts  11.2 us (2%)
    pallas_call x1, Pallas kernels, backward_sums(): pl.pallas_call(functools.partial(backward_kernel, n_steps, n_chunks, cols...  372 us
    pallas_call x1, Pallas kernels, forward_stack(): pl.pallas_call(forward_kernel, in_specs=[hbm] * 5, out_specs=hbm, out_sha...  178 us

profile of v3, /device:TPU:0, one launch (start us, length us, event | category | flops | bytes accessed | tf_op | source)
XLA Modules:
  0.0 588.6 jit_solution(3395551388432909714)
XLA Ops:
  0.6 371.9 %backward_reduce.1 = (f32[2,64,4096]{2,1,0:T(8,128)}, f32[2,256,1024]{2,1,0:T(8,128)}) custom-call(bf16[2,3072,1024]{2,1,0:T(8,128)(2,1)} %bitcast.25, bf16[3072,1024]{1,0:T(8,128)(2,1)} %bitcast.26, bf16[2,1024,4096]{2,1,0:T(8,128)(2,1)} %w1_hbm.1, bf16[2,16,8,32,1024]{4,3,2,1,0:T(8,128)(2,1)} %bitcast.24), custom_call_target="tpu_custom_call" | custom-call | flops 231928233984 | bytes 60000000 | tf_op jit(solution)/shard_map/backward_reduce/pallas_call | solution.py:291
  372.5 0.0 copy-start
  372.6 0.0 copy-start.4
  372.6 3.5 multiply_reduce_fusion.1
  376.1 0.0 copy-done
  376.1 0.0 copy-done.4
  376.1 2.4 multiply_reduce_fusion
  379.8 0.6 broadcast_in_dim.3.value_ref
  380.4 7.2 %norm_sum.1 = f32[8,128]{1,0:T(8,128)} custom-call(f32[8,128]{1,0:T(8,128)} %broadcast_in_dim.3.value_ref), custom_call_target="tpu_custom_call" | custom-call | tf_op jit(solution)/shard_map/norm_sum/pallas_call | solution.py:337
  387.7 1.2 slice.17
  389.6 0.0 copy-start.2
  389.6 0.0 copy-start.3
  389.6 7.7 %fusion.2 = (bf16[2,256,1024]{2,1,0:T(8,128)(2,1)S(1)}, f32[2,256,1024]{2,1,0:T(8,128)}, f32[2,256,1024]{2,1,0:T(8,128)}, f32[2,256,1024]{2,1,0:T(8,128)}) fusion(f32[2,256,1024]{2,1,0:T(8,128)} %param.21, f32[2,256,1024]{2,1,0:T(8,128)} %get-tuple-element.20, f32[]{:T(128)} %bitcast.4, f32[2,256,1024]{2,1,0:T(8,128)} %param.23, f32[2,256,1024]{2,1,0:T(8,128)} %param.25), kind=kLoop, calls=%fused_computation.13 | loop fusion | flops 8912896 | bytes 15728644 | tf_op jit(solution)/shard_map/convert_element_type | solution.py:545
  397.3 0.0 copy-start.1
  397.3 1.0 slice_bitcast_fusion
  398.4 0.0 copy-done.2
  398.4 0.0 copy-done.3
  398.4 0.9 copy-done.1
  399.3 3.8 fusion.4
  403.1 0.1 copy.23
  403.2 1.1 fusion.6
  404.3 178.1 %gather_forward.1 = bf16[3072,1024]{1,0:T(8,128)(2,1)} custom-call(bf16[3072,1024]{1,0:T(8,128)(2,1)} %bitcast.27, bf16[256,1024]{1,0:T(8,128)(2,1)} %bitcast.23, bf16[256,1024]{1,0:T(8,128)(2,1)} %get-tuple-element.24.down0_hbm, bf16[256,1024]{1,0:T(8,128)(2,1)} %bitcast.22, bf16[256,1024]{1,0:T(8,128)(2,1)} %get-tuple-element.23.down1_hbm), custom_call_target="tpu_custom_call" | custom-call | flops 103079215104 | bytes 20000000 | tf_op jit(solution)/shard_map/gather_forward/pallas_call | solution.py:519
  582.4 6.2 %copy.25 = bf16[2,1536,1024]{2,1,0:T(8,128)(2,1)} copy(bf16[2,1536,1024]{2,1,0:T(8,128)(2,1)} %bitcast.19) | data formatting | bytes 12582912
Async XLA Ops:
  372.5 3.6 copy-start
  372.6 3.5 copy-start.4
  389.6 8.8 %copy-start.2 = (f32[2,64,4096]{2,1,0:T(8,128)S(1)}, f32[2,64,4096]{2,1,0:T(8,128)}, u32[]{:S(2)}) copy-start(f32[2,64,4096]{2,1,0:T(8,128)} %param.22) | copy-start | bytes 6291460
  389.6 8.8 %copy-start.3 = (f32[2,64,4096]{2,1,0:T(8,128)S(1)}, f32[2,64,4096]{2,1,0:T(8,128)}, u32[]{:S(2)}) copy-start(f32[2,64,4096]{2,1,0:T(8,128)} %param.24) | copy-start | bytes 6291460
  397.3 2.0 copy-start.1

commit v4 on v3

--- a/solution.py
+++ b/solution.py
@@ -23,7 +23,7 @@
 TILE = 512
 LANES = 128
 ROWS = 128
-TILE_B = 384
+TILE_B = 512
 
 
 def adamw_update(master_old, mom_one, mom_two, grad_clip):
@@ -43,7 +43,7 @@
     return tuple(picks.get(dim, slice(None)) for dim in range(count))
 
 
-def backward_kernel(n_steps, n_chunks, cols, x_hbm, g_hbm, w1_hbm, w2_ref, out1_ref, out2_ref, x_buf, g_buf, x_turned, acc, act_turned, dh_buf, w1_group, w1_slots, part1, part2, *rest):
+def backward_kernel(n_steps, n_chunks, cols, x_hbm, g_hbm, w1_hbm, w2_ref, out1_ref, out2_ref, x_buf, g_buf, x_turned, acc, act_turned, dh_buf, w1_group, w1_ref, w1_next, part1, part2, *rest):
     parts = (part1, part2)
     recv0, send1, keep1, recv1, send2, keep2, recv2, send3, keep3, recv3 = (rest[2 * i:2 * i + 2] for i in range(10))
     load_sem, group_sem, send_sem0, recv_sem0, send_sem, recv_sem = rest[20:]
@@ -71,10 +71,8 @@
             send_sem=send_sem.at[slot], recv_sem=recv_sem.at[slot, lax.rem(block, 2)],
             device_id=(peers[ORDERS[color][phase - 1]],), device_id_type=MESH)
 
-    def each_color():
-        for mat in range(2):
-            for color in range(3):
-                yield mat, color, pl.ds(cols[mat][color][0], cols[mat][color][1] - cols[mat][color][0])
+    def colors(mat):
+        return [(color, pl.ds(lo, hi - lo)) for color, (lo, hi) in enumerate(cols[mat])]
 
     n_dev, per_dev = w2_ref.shape[:2]
     spread = LANES // per_dev
@@ -109,8 +107,6 @@
         load_x.start()
         load_x.wait()
 
-    w1_ref = w1_slots.at[lax.rem(step, 2)]
-
     def order_columns(rows, phase, target):
         part = lane_part()
         for tile in range(n_dev // spread):
@@ -127,9 +123,87 @@
             copy.wait()
 
         def row_body(block, carry):
-            order_columns(pl.ds(pl.multiple_of(block * ROWS, ROWS), ROWS), 0, w1_slots.at[0])
+            order_columns(pl.ds(pl.multiple_of(block * ROWS, ROWS), ROWS), 0, w1_next)
             return carry
         lax.fori_loop(0, x_buf.shape[1] // ROWS, row_body, 0)
+
+    def advance(mat):
+        @pl.when(step >= 4)
+        def _():
+            block = step - 4
+            for color, span in colors(mat):
+                copy = axis_copy(3, mat, color, block)
+                copy.wait_send()
+                copy.wait_recv()
+                total = keep3[mat][:, span] + recv3[mat][lax.rem(block, 2), :, span]
+                if mat == 1:
+                    out2_ref[:, span] = total
+                else:
+                    keep3[0][:, span] = total
+            if mat == 1:
+                return
+            chunk = lax.rem(block, n_chunks)
+
+            @pl.when(chunk == 0)
+            def _():
+                out1_ref[...] = jnp.zeros_like(out1_ref)
+            phase = lax.rem(chunk, spread)
+            part = lax.broadcasted_iota(jnp.int32, (out1_ref.shape[0], LANES), 1) // per_dev
+            for dev in range(n_dev):
+                tile = dev // spread
+                moved = pltpu.roll(keep3[0][:, tile * LANES:(tile + 1) * LANES], lax.rem(phase - dev % spread + spread, spread) * per_dev, 1)
+                spot = pl.ds(pl.multiple_of((dev * n_chunks // spread + chunk // spread) * LANES, LANES), LANES)
+                out1_ref[:, spot] = jnp.where(part == phase, moved, out1_ref[:, spot])
+
+        @pl.when((step >= 3) & (step < n_steps + 3))
+        def _():
+            block = step - 3
+            for color, span in colors(mat):
+                copy = axis_copy(2, mat, color, block)
+                copy.wait_send()
+                copy.wait_recv()
+                bit = bits[ORDERS[color][2]]
+                slot = lax.rem(block, 2)
+                send3[mat][:, span] = keep2[mat][1 - bit, :, span] + recv2[mat][slot, 1 - bit, :, span]
+                keep3[mat][:, span] = keep2[mat][bit, :, span] + recv2[mat][slot, bit, :, span]
+                axis_copy(3, mat, color, block).start()
+
+        @pl.when((step >= 2) & (step < n_steps + 2))
+        def _():
+            block = step - 2
+            for color, span in colors(mat):
+                copy = axis_copy(1, mat, color, block)
+                copy.wait_send()
+                copy.wait_recv()
+                left = [axis for axis in range(3) if axis != ORDERS[color][0]]
+                place = left.index(ORDERS[color][1])
+                bit = bits[ORDERS[color][1]]
+                slot = lax.rem(block, 2)
+                for value, store in ((1 - bit, send2), (bit, keep2)):
+                    index = at_bits({place: value}, 2)
+                    store[mat][:, :, span] = keep1[mat][index + (slice(None), span)] + recv1[mat][(slot,) + index + (slice(None), span)]
+                axis_copy(2, mat, color, block).start()
+
+        @pl.when((step >= 1) & (step < n_steps + 1))
+        def _():
+            block = step - 1
+            copy = core_copy(mat, block)
+            copy.wait_send()
+            copy.wait_recv()
+            for color, span in colors(mat):
+                axis = ORDERS[color][0]
+                slot = lax.rem(block, 2)
+                for value, store in ((1 - bits[axis], send1), (bits[axis], keep1)):
+                    index = at_bits({axis: value}, 3)
+                    mine = parts[mat][index + (bits[3], slice(None), span)].astype(jnp.float32)
+                    store[mat][:, :, :, span] = mine + recv0[mat][(slot,) + index + (slice(None), span)].astype(jnp.float32)
+                axis_copy(1, mat, color, block).start()
+
+    advance(0)
+
+    @pl.when(step < n_steps)
+    def _():
+        w1_ref[...] = w1_next[...]
 
     @pl.when((step < n_steps - 1) & (lax.rem(step, spread) == spread - 1))
     def _():
@@ -146,7 +220,6 @@
         act_turned[:, rows] = act.astype(jnp.bfloat16).T
         slope = gate + (act * (1.0 - gate)) * (2.0 * GELU_A + 6.0 * GELU_B * square)
         dh_buf[rows, :] = (d_act * slope).astype(jnp.bfloat16)
-        order_columns(pl.ds(pl.multiple_of(tile * ROWS, ROWS), ROWS), lax.rem(step + 1, spread), w1_slots.at[lax.rem(step + 1, 2)])
         if turn_x:
             x_turned[:, rows] = x_buf[rows, :].T
 
@@ -159,6 +232,13 @@
     @pl.when((step < n_steps) & (lax.rem(step, n_chunks) > 0))
     def _():
         lax.fori_loop(0, tokens // TILE_B, lambda tile, carry: (tile_body(tile, False), carry)[1], 0)
+
+    @pl.when(step < n_steps)
+    def _():
+        for block in range(w1_next.shape[0] // ROWS):
+            order_columns(pl.ds(block * ROWS, ROWS), lax.rem(step + 1, spread), w1_next)
+        part1[...] = jnp.dot(x_turned[...], dh_buf[...], preferred_element_type=jnp.float32).astype(jnp.bfloat16).reshape(part1.shape)
+        core_copy(0, step).start()
 
     @pl.when((step < n_steps - 2) & (lax.rem(step, spread) == spread - 2))
     def _():
@@ -166,82 +246,12 @@
         for copy in group_copies(w1_hbm.shape[0] - 1 - following // n_chunks, lax.rem(following, n_chunks) // spread):
             copy.start()
 
-    @pl.when(step >= 4)
-    def _():
-        block = step - 4
-        for mat, color, span in each_color():
-            copy = axis_copy(3, mat, color, block)
-            copy.wait_send()
-            copy.wait_recv()
-            total = keep3[mat][:, span] + recv3[mat][lax.rem(block, 2), :, span]
-            if mat == 1:
-                out2_ref[:, span] = total
-            else:
-                keep3[0][:, span] = total
-        chunk = lax.rem(block, n_chunks)
-
-        @pl.when(chunk == 0)
-        def _():
-            out1_ref[...] = jnp.zeros_like(out1_ref)
-        phase = lax.rem(chunk, spread)
-        part = lax.broadcasted_iota(jnp.int32, (out1_ref.shape[0], LANES), 1) // per_dev
-        for dev in range(n_dev):
-            tile = dev // spread
-            moved = pltpu.roll(keep3[0][:, tile * LANES:(tile + 1) * LANES], lax.rem(phase - dev % spread + spread, spread) * per_dev, 1)
-            spot = pl.ds(pl.multiple_of((dev * n_chunks // spread + chunk // spread) * LANES, LANES), LANES)
-            out1_ref[:, spot] = jnp.where(part == phase, moved, out1_ref[:, spot])
-
-    @pl.when((step >= 3) & (step < n_steps + 3))
-    def _():
-        block = step - 3
-        for mat, color, span in each_color():
-            copy = axis_copy(2, mat, color, block)
-            copy.wait_send()
-            copy.wait_recv()
-            bit = bits[ORDERS[color][2]]
-            slot = lax.rem(block, 2)
-            send3[mat][:, span] = keep2[mat][1 - bit, :, span] + recv2[mat][slot, 1 - bit, :, span]
-            keep3[mat][:, span] = keep2[mat][bit, :, span] + recv2[mat][slot, bit, :, span]
-            axis_copy(3, mat, color, block).start()
-
-    @pl.when((step >= 2) & (step < n_steps + 2))
-    def _():
-        block = step - 2
-        for mat, color, span in each_color():
-            copy = axis_copy(1, mat, color, block)
-            copy.wait_send()
-            copy.wait_recv()
-            left = [axis for axis in range(3) if axis != ORDERS[color][0]]
-            place = left.index(ORDERS[color][1])
-            bit = bits[ORDERS[color][1]]
-            slot = lax.rem(block, 2)
-            for value, store in ((1 - bit, send2), (bit, keep2)):
-                index = at_bits({place: value}, 2)
-                store[mat][:, :, span] = keep1[mat][index + (slice(None), span)] + recv1[mat][(slot,) + index + (slice(None), span)]
-            axis_copy(2, mat, color, block).start()
-
-    @pl.when((step >= 1) & (step < n_steps + 1))
-    def _():
-        block = step - 1
-        for mat in range(2):
-            copy = core_copy(mat, block)
-            copy.wait_send()
-            copy.wait_recv()
-        for mat, color, span in each_color():
-            axis = ORDERS[color][0]
-            slot = lax.rem(block, 2)
-            for value, store in ((1 - bits[axis], send1), (bits[axis], keep1)):
-                index = at_bits({axis: value}, 3)
-                mine = parts[mat][index + (bits[3], slice(None), span)].astype(jnp.float32)
-                store[mat][:, :, :, span] = mine + recv0[mat][(slot,) + index + (slice(None), span)].astype(jnp.float32)
-            axis_copy(1, mat, color, block).start()
+    advance(1)
 
     @pl.when(step < n_steps)
     def _():
         part2[...] = jnp.dot(act_turned[...], g_buf[...], preferred_element_type=jnp.float32).astype(jnp.bfloat16).reshape(part2.shape)
         core_copy(1, step).start()
-        part1[...] = jnp.dot(x_turned[...], dh_buf[...], preferred_element_type=jnp.float32).astype(jnp.bfloat16).reshape(part1.shape)
-        core_copy(0, step).start()
 
     @pl.when(step < n_chunks)
     def _():
@@ -281,7 +291,7 @@
     f32, b16 = jnp.float32, jnp.bfloat16
     scratch = [pltpu.VMEM((tokens, model_width), b16), pltpu.VMEM((tokens, model_width), b16), pltpu.VMEM((model_width, tokens), b16),
                pltpu.VMEM((tokens, model_width), f32), pltpu.VMEM((chunk, tokens), b16), pltpu.VMEM((tokens, chunk), b16),
-               pltpu.VMEM((n_dev, model_width, LANES), b16), pltpu.VMEM((2, model_width, chunk), b16)]
+               pltpu.VMEM((n_dev, model_width, LANES), b16), pltpu.VMEM((model_width, chunk), b16), pltpu.VMEM((model_width, chunk), b16)]
     scratch += pair((2, 2, 2, 2), b16) + pair((2, 2, 2, 2), b16)
     for lead in ((2, 2), (2,), ()):
         scratch += pair(lead, f32) + pair(lead, f32) + pair((2,) + lead, f32)
@@ -426,13 +436,13 @@
     load(1).wait()
     load(2).wait()
     second(0)
+    start(2, 0)
     second(1)
     third(0)
-    start(2, 0)
-    hand_over(0)
-    third(1)
     second(2)
     start(3, 0)
+    third(1)
+    hand_over(0)
     load_x.wait()
     complete(0)
 
@@ -469,20 +479,12 @@
         down(tile, matrix)
         store(tile).start()
 
-    def event_second():
-        hand_over(1)
+    def widen_both():
+        second(3)
         third(2)
-        second(3)
-
-    def event_third():
-        hand_over(2)
-        third(3)
-
-    def event_fourth():
-        hand_over(3)
-        third(4)
-
-    run(4 * n_tiles, 0, up, {2 * n_tiles - 1: event_second, 2 * n_tiles: lambda: complete(1), 4 * n_tiles - 1: event_third})
+
+    run(4 * n_tiles, 0, up, {3: widen_both, 2 * n_tiles - 3: lambda: hand_over(1), 2 * n_tiles: lambda: complete(1),
+                             3 * n_tiles: lambda: third(3), 4 * n_tiles - 1: lambda: hand_over(2)})
     for piece in (0, 1):
         for phase in range(5):
             for copy in copies(piece, phase):
@@ -494,9 +496,9 @@
     load(3).wait()
     pl.semaphore_wait(free_sem, 4)
     start(4, 0)
-    run(n_tiles, 1, down, {2: lambda: second(4), n_tiles - 1: event_fourth})
+    run(n_tiles, 1, down, {n_tiles - 2: lambda: hand_over(3), n_tiles - 1: lambda: second(4)})
     complete(3)
-    run(4 * n_tiles, 2, up, {4 * n_tiles - 3: lambda: hand_over(4)})
+    run(4 * n_tiles, 2, up, {n_tiles: lambda: third(4), 4 * n_tiles - 2: lambda: hand_over(4)})
     complete(4)
     run(n_tiles, 3, down_last, {})
     for piece in (2, 3, 4):

time: 589 us -> 565 us (0.959)
  Pallas kernels: 557 us -> 533 us
    pallas_call x1, Pallas kernels: 372 us -> 357 us  [backward_sums(): pl.pallas_call(functools.partial(backward_kernel, n_steps, n_chunks, cols...]
    pallas_call x1, Pallas kernels: 178 us -> 169 us  [forward_stack(): pl.pallas_call(forward_kernel, in_specs=[hbm] * 5, out_specs=hbm, out_sha...]
where the time goes in v4:
time: 565 us
  Pallas kernels  533 us (94%)
  other arithmetic  17.6 us (3%)
  local copies, waits for them, and re-layouts  11.2 us (2%)
    pallas_call x1, Pallas kernels, backward_sums(): pl.pallas_call(functools.partial(backward_kernel, n_steps, n_chunks, cols...  357 us
    pallas_call x1, Pallas kernels, forward_stack(): pl.pallas_call(forward_kernel, in_specs=[hbm] * 5, out_specs=hbm, out_sha...  169 us

profile of v4, /device:TPU:0, one launch (start us, length us, event | category | flops | bytes accessed | tf_op | source)
XLA Modules:
  0.0 564.5 jit_solution(9555836340250136941)
XLA Ops:
  0.6 357.2 %backward_reduce.1 = (f32[2,64,4096]{2,1,0:T(8,128)}, f32[2,256,1024]{2,1,0:T(8,128)}) custom-call(bf16[2,3072,1024]{2,1,0:T(8,128)(2,1)} %bitcast.25, bf16[3072,1024]{1,0:T(8,128)(2,1)} %bitcast.26, bf16[2,1024,4096]{2,1,0:T(8,128)(2,1)} %w1_hbm.1, bf16[2,16,8,32,1024]{4,3,2,1,0:T(8,128)(2,1)} %bitcast.24), custom_call_target="tpu_custom_call" | custom-call | flops 231928233984 | bytes 60000000 | tf_op jit(solution)/shard_map/backward_reduce/pallas_call | solution.py:301
  357.8 0.0 copy-start
  357.8 0.0 copy-start.4
  357.8 3.5 multiply_reduce_fusion.1
  361.3 0.0 copy-done
  361.4 0.0 copy-done.4
  361.4 2.4 multiply_reduce_fusion
  365.1 0.6 broadcast_in_dim.3.value_ref
  365.7 7.3 %norm_sum.1 = f32[8,128]{1,0:T(8,128)} custom-call(f32[8,128]{1,0:T(8,128)} %broadcast_in_dim.3.value_ref), custom_call_target="tpu_custom_call" | custom-call | tf_op jit(solution)/shard_map/norm_sum/pallas_call | solution.py:347
  373.0 1.2 slice.17
  374.9 0.0 copy-start.2
  374.9 0.0 copy-start.3
  374.9 7.7 %fusion.2 = (bf16[2,256,1024]{2,1,0:T(8,128)(2,1)S(1)}, f32[2,256,1024]{2,1,0:T(8,128)}, f32[2,256,1024]{2,1,0:T(8,128)}, f32[2,256,1024]{2,1,0:T(8,128)}) fusion(f32[2,256,1024]{2,1,0:T(8,128)} %param.21, f32[2,256,1024]{2,1,0:T(8,128)} %get-tuple-element.20, f32[]{:T(128)} %bitcast.4, f32[2,256,1024]{2,1,0:T(8,128)} %param.23, f32[2,256,1024]{2,1,0:T(8,128)} %param.25), kind=kLoop, calls=%fused_computation.13 | loop fusion | flops 8912896 | bytes 15728644 | tf_op jit(solution)/shard_map/convert_element_type | solution.py:547
  382.7 0.0 copy-start.1
  382.7 1.0 slice_bitcast_fusion
  383.7 0.0 copy-done.2
  383.7 0.0 copy-done.3
  383.7 0.9 copy-done.1
  384.6 3.8 fusion.4
  388.5 0.1 copy.23
  388.6 1.1 fusion.6
  389.7 168.6 %gather_forward.1 = bf16[3072,1024]{1,0:T(8,128)(2,1)} custom-call(bf16[3072,1024]{1,0:T(8,128)(2,1)} %bitcast.27, bf16[256,1024]{1,0:T(8,128)(2,1)} %bitcast.23, bf16[256,1024]{1,0:T(8,128)(2,1)} %get-tuple-element.24.down0_hbm, bf16[256,1024]{1,0:T(8,128)(2,1)} %bitcast.22, bf16[256,1024]{1,0:T(8,128)(2,1)} %get-tuple-element.23.down1_hbm), custom_call_target="tpu_custom_call" | custom-call | flops 103079215104 | bytes 20000000 | tf_op jit(solution)/shard_map/gather_forward/pallas_call | solution.py:521
  558.3 6.2 %copy.25 = bf16[2,1536,1024]{2,1,0:T(8,128)(2,1)} copy(bf16[2,1536,1024]{2,1,0:T(8,128)(2,1)} %bitcast.19) | data formatting | bytes 12582912
Async XLA Ops:
  357.8 3.6 copy-start
  357.8 3.5 copy-start.4
  374.9 8.8 %copy-start.2 = (f32[2,64,4096]{2,1,0:T(8,128)S(1)}, f32[2,64,4096]{2,1,0:T(8,128)}, u32[]{:S(2)}) copy-start(f32[2,64,4096]{2,1,0:T(8,128)} %param.22) | copy-start | bytes 6291460
  374.9 8.8 %copy-start.3 = (f32[2,64,4096]{2,1,0:T(8,128)S(1)}, f32[2,64,4096]{2,1,0:T(8,128)}, u32[]{:S(2)}) copy-start(f32[2,64,4096]{2,1,0:T(8,128)} %param.24) | copy-start | bytes 6291460
  382.7 2.0 copy-start.1

commit v5 on v4

--- a/solution.py
+++ b/solution.py
@@ -13,7 +13,6 @@
 ADAM_EPS = 1e-8
 WEIGHT_DECAY = 0.1
 ADAM_STEP = 3
-MICRO_STEPS = 2
 
 GELU_A = math.sqrt(2.0 / math.pi)
 GELU_B = GELU_A * 0.044715
@@ -43,10 +42,11 @@
     return tuple(picks.get(dim, slice(None)) for dim in range(count))
 
 
-def backward_kernel(n_steps, n_chunks, cols, x_hbm, g_hbm, w1_hbm, w2_ref, out1_ref, out2_ref, x_buf, g_buf, x_turned, acc, act_turned, dh_buf, w1_group, w1_ref, w1_next, part1, part2, *rest):
+def backward_kernel(n_steps, n_chunks, cols, x_hbm, g_hbm, w1_hbm, w2_ref, gacc1_hbm, gacc2_ref, out1_block, out2_ref, norm_ref, x_buf, g_buf, x_turned, acc, act_turned, dh_buf, w1_group, w1_ref, w1_next, part1, part2, *rest):
     parts = (part1, part2)
+    out1_ref = out1_block.at[0]
     recv0, send1, keep1, recv1, send2, keep2, recv2, send3, keep3, recv3 = (rest[2 * i:2 * i + 2] for i in range(10))
-    load_sem, group_sem, send_sem0, recv_sem0, send_sem, recv_sem = rest[20:]
+    squares, gathered, load_sem, group_sem, send_sem0, recv_sem0, send_sem, recv_sem, norm_send, norm_recv = rest[20:]
     step = pl.program_id(0)
     me = lax.axis_index("fsdp")
     bits = [lax.rem(me // stride, 2) for stride in STRIDES]
@@ -85,28 +85,6 @@
             w1_hbm.at[layer, :, pl.ds(pl.multiple_of((dev * n_chunks // spread + half) * LANES, LANES), LANES)],
             w1_group.at[dev], group_sem.at[dev]) for dev in range(n_dev)]
 
-    @pl.when(step == 0)
-    def _():
-        for copy in group_copies(w1_hbm.shape[0] - 1, 0):
-            copy.start()
-        barrier = pltpu.get_barrier_semaphore()
-        for peer in peers:
-            pl.semaphore_signal(barrier, inc=1, device_id=(peer,), device_id_type=MESH)
-        load_x = pltpu.make_async_copy(x_hbm.at[1], x_buf, load_sem.at[0])
-        load_g = pltpu.make_async_copy(g_hbm, g_buf, load_sem.at[1])
-        load_x.start()
-        load_g.start()
-        acc[...] = jnp.zeros_like(acc)
-        load_x.wait()
-        load_g.wait()
-        pl.semaphore_wait(barrier, 4)
-
-    @pl.when(step == n_chunks)
-    def _():
-        load_x = pltpu.make_async_copy(x_hbm.at[0], x_buf, load_sem.at[0])
-        load_x.start()
-        load_x.wait()
-
     def order_columns(rows, phase, target):
         part = lane_part()
         for tile in range(n_dev // spread):
@@ -119,6 +97,17 @@
 
     @pl.when(step == 0)
     def _():
+        for copy in group_copies(w1_hbm.shape[0] - 1, 0):
+            copy.start()
+        load_x = pltpu.make_async_copy(x_hbm.at[w1_hbm.shape[0] - 1], x_buf, load_sem.at[0])
+        load_g = pltpu.make_async_copy(g_hbm, g_buf, load_sem.at[1])
+        load_x.start()
+        load_g.start()
+        barrier = pltpu.get_barrier_semaphore()
+        for shift in range(1, n_dev):
+            pl.semaphore_signal(barrier, inc=1, device_id=(lax.rem(me + shift, n_dev),), device_id_type=MESH)
+        acc[...] = jnp.zeros_like(acc)
+        squares[...] = jnp.zeros_like(squares)
         for copy in group_copies(0, 0):
             copy.wait()
 
@@ -126,6 +115,24 @@
             order_columns(pl.ds(pl.multiple_of(block * ROWS, ROWS), ROWS), 0, w1_next)
             return carry
         lax.fori_loop(0, x_buf.shape[1] // ROWS, row_body, 0)
+        load_x.wait()
+        load_g.wait()
+        pl.semaphore_wait(barrier, n_dev - 1)
+
+    def next_x():
+        return pltpu.make_async_copy(x_hbm.at[0], x_buf, load_sem.at[0])
+
+    @pl.when(step == n_chunks)
+    def _():
+        next_x().wait()
+
+    def add_squares(grad):
+        total = squares[...]
+        for row in range(0, grad.shape[0], 8):
+            for lane in range(0, grad.shape[1], LANES):
+                piece = grad[row:row + 8, lane:lane + LANES]
+                total = total + piece * piece
+        squares[...] = total
 
     def advance(mat):
         @pl.when(step >= 4)
@@ -137,7 +144,9 @@
                 copy.wait_recv()
                 total = keep3[mat][:, span] + recv3[mat][lax.rem(block, 2), :, span]
                 if mat == 1:
-                    out2_ref[:, span] = total
+                    grad = 0.5 * (gacc2_ref[:, span] + total)
+                    out2_ref[:, span] = grad
+                    add_squares(grad)
                 else:
                     keep3[0][:, span] = total
             if mat == 1:
@@ -146,14 +155,20 @@
 
             @pl.when(chunk == 0)
             def _():
-                out1_ref[...] = jnp.zeros_like(out1_ref)
+                load = pltpu.make_async_copy(gacc1_hbm.at[w1_hbm.shape[0] - 1 - block // n_chunks], out1_ref, load_sem.at[2])
+                load.start()
+                load.wait()
             phase = lax.rem(chunk, spread)
             part = lax.broadcasted_iota(jnp.int32, (out1_ref.shape[0], LANES), 1) // per_dev
             for dev in range(n_dev):
                 tile = dev // spread
                 moved = pltpu.roll(keep3[0][:, tile * LANES:(tile + 1) * LANES], lax.rem(phase - dev % spread + spread, spread) * per_dev, 1)
                 spot = pl.ds(pl.multiple_of((dev * n_chunks // spread + chunk // spread) * LANES, LANES), LANES)
-                out1_ref[:, spot] = jnp.where(part == phase, moved, out1_ref[:, spot])
+                out1_ref[:, spot] = jnp.where(part == phase, 0.5 * (out1_ref[:, spot] + moved), out1_ref[:, spot])
+
+            @pl.when(chunk == n_chunks - 1)
+            def _():
+                add_squares(out1_ref[...])
 
         @pl.when((step >= 3) & (step < n_steps + 3))
         def _():
@@ -240,6 +255,10 @@
         part1[...] = jnp.dot(x_turned[...], dh_buf[...], preferred_element_type=jnp.float32).astype(jnp.bfloat16).reshape(part1.shape)
         core_copy(0, step).start()
 
+    @pl.when(step == n_chunks - 1)
+    def _():
+        next_x().start()
+
     @pl.when((step < n_steps - 2) & (lax.rem(step, spread) == spread - 2))
     def _():
         following = step + 2
@@ -269,8 +288,27 @@
             return carry
         lax.fori_loop(0, tokens // TILE, tile_body, 0)
 
-
-def backward_sums(x_tokens, grad_tokens, w_up, w_down, n_dev):
+    @pl.when(step == n_steps + 3)
+    def _():
+        def copy_of(shift, sender):
+            return pltpu.make_async_remote_copy(
+                src_ref=squares, dst_ref=gathered.at[sender], send_sem=norm_send.at[shift], recv_sem=norm_recv.at[sender],
+                device_id=(lax.rem(me + shift, n_dev),), device_id_type=MESH)
+
+        for shift in range(1, n_dev):
+            copy_of(shift, me).start()
+        gathered[me] = squares[...]
+        for shift in range(1, n_dev):
+            copy_of(shift, lax.rem(me + n_dev - shift, n_dev)).wait_recv()
+        total = gathered[0]
+        for dev in range(1, n_dev):
+            total = total + gathered[dev]
+        norm_ref[...] = jnp.broadcast_to(jnp.sum(total, keepdims=True), norm_ref.shape)
+        for shift in range(1, n_dev):
+            copy_of(shift, me).wait_send()
+
+
+def backward_grads(x_tokens, grad_tokens, w_up, w_down, gacc_up, gacc_down, n_dev):
     layers, model_width, ff_width = w_up.shape
     tokens = grad_tokens.shape[0]
     chunk = 512
@@ -296,60 +334,27 @@
     for lead in ((2, 2), (2,), ()):
         scratch += pair(lead, f32) + pair(lead, f32) + pair((2,) + lead, f32)
     dma = pltpu.SemaphoreType.DMA
-    scratch += [dma((2,)), dma((n_dev,)), dma((2,)), dma((2, 2)), dma((18,)), dma((18, 2))]
+    scratch += [pltpu.VMEM((8, LANES), f32), pltpu.VMEM((n_dev, 8, LANES), f32)]
+    scratch += [dma((3,)), dma((n_dev,)), dma((2,)), dma((2, 2)), dma((18,)), dma((18, 2)), dma((n_dev,)), dma((n_dev,))]
     hbm = pl.BlockSpec(memory_space=pl.ANY)
-    out1, out2 = pl.pallas_call(
+    grad_up, grad_down, norm_sq = pl.pallas_call(
         functools.partial(backward_kernel, n_steps, n_chunks, cols),
         grid=(n_steps + 4,),
         in_specs=[hbm, hbm,
                   hbm,
-                  pl.BlockSpec((None, n_dev, None, per_dev, model_width), lambda s: (where(s)[0], 0, where(s)[1], 0, 0))],
-        out_specs=[pl.BlockSpec((None, rows_up, ff_width), lambda s: (where(jnp.maximum(s - 4, 0))[0], 0, 0)),
-                   pl.BlockSpec((None, per_dev, model_width), lambda s: (*where(jnp.maximum(s - 4, 0)), 0))],
-        out_shape=[jax.ShapeDtypeStruct((layers, rows_up, ff_width), f32), jax.ShapeDtypeStruct((layers, n_chunks * per_dev, model_width), f32)],
+                  pl.BlockSpec((None, n_dev, None, per_dev, model_width), lambda s: (where(s)[0], 0, where(s)[1], 0, 0)),
+                  hbm, pl.BlockSpec((None, per_dev, model_width), lambda s: (*where(jnp.maximum(s - 4, 0)), 0))],
+        out_specs=[pl.BlockSpec((1, rows_up, ff_width), lambda s: (where(jnp.maximum(s - 4, 0))[0], 0, 0)),
+                   pl.BlockSpec((None, per_dev, model_width), lambda s: (*where(jnp.maximum(s - 4, 0)), 0)),
+                   pl.BlockSpec((8, LANES), lambda s: (0, 0))],
+        out_shape=[jax.ShapeDtypeStruct((layers, rows_up, ff_width), f32), jax.ShapeDtypeStruct((layers, n_chunks * per_dev, model_width), f32),
+                   jax.ShapeDtypeStruct((8, LANES), f32)],
         scratch_shapes=scratch,
         compiler_params=pltpu.CompilerParams(vmem_limit_bytes=67_043_328, dimension_semantics=("arbitrary",), collective_id=0, has_side_effects=True),
         cost_estimate=pl.CostEstimate(flops=18 * tokens * model_width * ff_width, bytes_accessed=60_000_000, transcendentals=2 * tokens * ff_width),
         name="backward_reduce",
-    )(x_tokens, grad_tokens, w_up, w2_view)
-    return out1, out2
-
-
-def norm_kernel(n_dev, value_ref, out_ref, gathered, send_sem, recv_sem):
-    me = lax.axis_index("fsdp")
-    barrier = pltpu.get_barrier_semaphore()
-    for shift in range(1, n_dev):
-        pl.semaphore_signal(barrier, inc=1, device_id=(lax.rem(me + shift, n_dev),), device_id_type=MESH)
-    pl.semaphore_wait(barrier, n_dev - 1)
-
-    def copy_of(shift, sender):
-        return pltpu.make_async_remote_copy(
-            src_ref=value_ref, dst_ref=gathered.at[sender], send_sem=send_sem.at[shift], recv_sem=recv_sem.at[sender],
-            device_id=(lax.rem(me + shift, n_dev),), device_id_type=MESH)
-
-    for shift in range(1, n_dev):
-        copy_of(shift, me).start()
-    gathered[me] = value_ref[...]
-    for shift in range(1, n_dev):
-        copy_of(shift, lax.rem(me + n_dev - shift, n_dev)).wait_recv()
-    total = gathered[0]
-    for dev in range(1, n_dev):
-        total = total + gathered[dev]
-    out_ref[...] = total
-    for shift in range(1, n_dev):
-        copy_of(shift, me).wait_send()
-
-
-def global_sum(value, n_dev):
-    tile = jnp.broadcast_to(value, (8, LANES))
-    vmem = pl.BlockSpec(memory_space=pltpu.VMEM)
-    dma = pltpu.SemaphoreType.DMA
-    return pl.pallas_call(
-        functools.partial(norm_kernel, n_dev), in_specs=[vmem], out_specs=vmem,
-        out_shape=jax.ShapeDtypeStruct(tile.shape, jnp.float32),
-        scratch_shapes=[pltpu.VMEM((n_dev,) + tile.shape, jnp.float32), dma((n_dev,)), dma((n_dev,))],
-        compiler_params=pltpu.CompilerParams(collective_id=1, has_side_effects=True),
-        name="norm_sum")(tile)[0, 0]
+    )(x_tokens, grad_tokens, w_up, w2_view, gacc_up, gacc_down)
+    return grad_up, grad_down, norm_sq[0, 0]
 
 
 def forward_kernel(x_hbm, up0_hbm, down0_hbm, up1_hbm, down1_hbm, y_hbm, h_buf, act_buf, buf_a, buf_b, buf_c, load_sem, free_sem, send_sem, recv_sem):
@@ -523,7 +528,7 @@
         out_shape=jax.ShapeDtypeStruct((tokens, model_width), b16),
         scratch_shapes=[pltpu.VMEM((tokens, model_width), b16), pltpu.VMEM((blocks, tokens, model_width), b16), gathered, gathered, gathered,
                         dma((5 + tokens // TILE,)), pltpu.SemaphoreType.REGULAR, dma((75,)), dma((75,))],
-        compiler_params=pltpu.CompilerParams(vmem_limit_bytes=67_043_328, collective_id=2, has_side_effects=True),
+        compiler_params=pltpu.CompilerParams(vmem_limit_bytes=67_043_328, collective_id=1, has_side_effects=True),
         cost_estimate=pl.CostEstimate(flops=8 * tokens * model_width * ff_width, bytes_accessed=20_000_000, transcendentals=2 * tokens * ff_width),
         name="gather_forward",
     )(x_tokens, up_blocks[0], down_shard[0], up_blocks[1], down_shard[1])
@@ -536,11 +541,8 @@
     def local_step(x_saved, grad_out, x_next, w_up, w_down, gacc_up, gacc_down, master_up, master_down, mom1_up, mom1_down, mom2_up, mom2_down):
         layers, model_width, ff_width = w_up.shape
         clip_norm = 0.1 * math.sqrt(2 * layers * model_width * ff_width)
-        sums_up, sums_down = backward_sums(x_saved.reshape(layers, -1, model_width), grad_out.reshape(-1, model_width), w_up, w_down, n_dev)
-        grad_up = (gacc_up + sums_up) / MICRO_STEPS
-        grad_down = (gacc_down + sums_down) / MICRO_STEPS
-        local_sq = jnp.sum(grad_up * grad_up) + jnp.sum(grad_down * grad_down)
-        clip_factor = jnp.minimum(1.0, clip_norm / jnp.sqrt(global_sum(local_sq, n_dev)))
+        grad_up, grad_down, norm_sq = backward_grads(x_saved.reshape(layers, -1, model_width), grad_out.reshape(-1, model_width), w_up, w_down, gacc_up, gacc_down, n_dev)
+        clip_factor = jnp.minimum(1.0, clip_norm / jnp.sqrt(norm_sq))
         new_up = adamw_update(master_up, mom1_up, mom2_up, grad_up * clip_factor)
         new_down = adamw_update(master_down, mom1_down, mom2_down, grad_down * clip_factor)
         up_shard = new_up[0].astype(jnp.bfloat16)

time: 565 us -> 556 us (0.984)
  other arithmetic: 17.6 us -> 11.4 us
    reduce_sum x2 -> x0, other arithmetic: 5.98 us -> none  [local_step(): local_sq = jnp.sum(grad_up * grad_up) + jnp.sum(grad_down * grad_down)]
    pallas_call x2 -> x1, Pallas kernels: 364 us -> 363 us  [backward_grads(): pl.pallas_call(functools.partial(backward_kernel, n_steps, n_chunks, cols...]
where the time goes in v5:
time: 556 us
  Pallas kernels  532 us (96%)
  other arithmetic  11.4 us (2%)
  local copies, waits for them, and re-layouts  11 us (2%)
    pallas_call x1, Pallas kernels, backward_grads(): pl.pallas_call(functools.partial(backward_kernel, n_steps, n_chunks, cols...  363 us
    pallas_call x1, Pallas kernels, forward_stack(): pl.pallas_call(forward_kernel, in_specs=[hbm] * 5, out_specs=hbm, out_sha...  169 us

profile of v5, /device:TPU:0, one launch (start us, length us, event | category | flops | bytes accessed | tf_op | source)
XLA Modules:
  0.0 555.5 jit_solution(15472420052761986495)
XLA Ops:
  0.6 362.8 %backward_reduce.1 = (f32[2,64,4096]{2,1,0:T(8,128)}, f32[2,256,1024]{2,1,0:T(8,128)}, f32[8,128]{1,0:T(8,128)}) custom-call(bf16[2,3072,1024]{2,1,0:T(8,128)(2,1)} %bitcast.25, bf16[3072,1024]{1,0:T(8,128)(2,1)} %bitcast.26, bf16[2,1024,4096]{2,1,0:T(8,128)(2,1)} %w1_hbm.1, bf16[2,16,8,32,1024]{4,3,2,1,0:T(8,128)(2,1)} %bitcast.24, ...), custom_call_target="tpu_custom_call" | custom-call | flops 231928233984 | bytes 60000000 | tf_op jit(solution)/shard_map/backward_reduce/pallas_call | solution.py:340
  363.4 1.2 slice.17
  365.3 0.0 copy-start.2
  365.3 0.0 copy-start.3
  365.3 7.5 %fusion.4 = (bf16[2,64,4096]{2,1,0:T(8,128)(2,1)S(1)}, f32[2,64,4096]{2,1,0:T(8,128)}, f32[2,64,4096]{2,1,0:T(8,128)}, f32[2,64,4096]{2,1,0:T(8,128)}) fusion(f32[2,64,4096]{2,1,0:T(8,128)} %param.20, f32[2,64,4096]{2,1,0:T(8,128)} %get-tuple-element.10, f32[]{:T(128)} %bitcast.4, f32[2,64,4096]{2,1,0:T(8,128)} %param.22, f32[2,64,4096]{2,1,0:T(8,128)} %param.24), kind=kLoop, calls=%fused_computation.12 | loop fusion | flops 8912896 | bytes 15728644 | tf_op jit(solution)/shard_map/convert_element_type | solution.py:548
  372.9 0.0 copy-start
  372.9 0.0 copy-start.1
  372.9 0.1 copy.23
  372.9 1.1 fusion.6
  374.0 0.0 copy-done.2
  374.0 0.0 copy-done.3
  374.0 0.8 copy-done
  374.8 0.6 copy-done.1
  375.5 3.9 fusion.2
  379.4 1.0 slice_bitcast_fusion
  380.4 168.9 %gather_forward.1 = bf16[3072,1024]{1,0:T(8,128)(2,1)} custom-call(bf16[3072,1024]{1,0:T(8,128)(2,1)} %bitcast.27, bf16[256,1024]{1,0:T(8,128)(2,1)} %bitcast.23, bf16[256,1024]{1,0:T(8,128)(2,1)} %get-tuple-element.22.down0_hbm, bf16[256,1024]{1,0:T(8,128)(2,1)} %bitcast.22, bf16[256,1024]{1,0:T(8,128)(2,1)} %get-tuple-element.21.down1_hbm), custom_call_target="tpu_custom_call" | custom-call | flops 103079215104 | bytes 20000000 | tf_op jit(solution)/shard_map/gather_forward/pallas_call | solution.py:526
  549.3 6.2 %copy.25 = bf16[2,1536,1024]{2,1,0:T(8,128)(2,1)} copy(bf16[2,1536,1024]{2,1,0:T(8,128)(2,1)} %bitcast.19) | data formatting | bytes 12582912
Async XLA Ops:
  365.3 8.7 %copy-start.2 = (f32[2,256,1024]{2,1,0:T(8,128)S(1)}, f32[2,256,1024]{2,1,0:T(8,128)}, u32[]{:S(2)}) copy-start(f32[2,256,1024]{2,1,0:T(8,128)} %param.25) | copy-start | bytes 6291460
  365.3 8.7 %copy-start.3 = (f32[2,256,1024]{2,1,0:T(8,128)S(1)}, f32[2,256,1024]{2,1,0:T(8,128)}, u32[]{:S(2)}) copy-start(f32[2,256,1024]{2,1,0:T(8,128)} %get-tuple-element.12) | copy-start | bytes 6291460
  372.9 2.0 copy-start
  372.9 2.6 copy-start.1

commit v6 on v5

--- a/solution.py
+++ b/solution.py
@@ -371,28 +371,25 @@
 
     def spans(piece):
         _, lo, hi = pieces[piece]
-        size = (hi - lo) // 16
-        third = size // 3
-        cuts = [0, third, 2 * third, size]
-        if piece % 3 == 1:
-            cuts = [0, third, size - third, size]
-        if piece % 3 == 2:
-            cuts = [0, size - 2 * third, size - third, size]
-        return [(lo + 16 * cuts[color], 16 * (cuts[color + 1] - cuts[color])) for color in range(3)]
+        third = (hi - lo) // 48 * 16
+        rest = lo + 3 * third
+        cuts = (0, 3 * width // 8, 3 * width // 4, width)
+        return ([(color, lo + color * third, third, 0, width) for color in range(3)]
+                + [(color, rest, hi - rest, cuts[color], cuts[color + 1] - cuts[color]) for color in range(3)])
 
     def copies(piece, phase):
         matrix = pieces[piece][0]
         out = []
-        for color, (lo, size) in enumerate(spans(piece)):
+        for index, (color, lo, size, left, breadth) in enumerate(spans(piece)):
             order = ORDERS[color]
             picks = {axis: bits[axis] for axis in range(4)}
             for axis in order[:min(phase, 2)]:
                 picks.pop(axis)
             if phase == 4:
                 picks[order[2]] = 1 - bits[order[2]]
-            where = at_bits(picks, 4) + (pl.ds(lo, size),)
+            where = at_bits(picks, 4) + (pl.ds(lo, size), pl.ds(left, breadth))
             axis = order[phase] if phase < 3 else 3
-            slot = (piece * 5 + phase) * 3 + color
+            slot = (piece * 5 + phase) * 6 + index
             out.append(pltpu.make_async_remote_copy(
                 src_ref=bufs[matrix].at[where], dst_ref=bufs[matrix].at[where],
                 send_sem=send_sem.at[slot], recv_sem=recv_sem.at[slot],
@@ -527,7 +524,7 @@
         forward_kernel, in_specs=[hbm] * 5, out_specs=hbm,
         out_shape=jax.ShapeDtypeStruct((tokens, model_width), b16),
         scratch_shapes=[pltpu.VMEM((tokens, model_width), b16), pltpu.VMEM((blocks, tokens, model_width), b16), gathered, gathered, gathered,
-                        dma((5 + tokens // TILE,)), pltpu.SemaphoreType.REGULAR, dma((75,)), dma((75,))],
+                        dma((5 + tokens // TILE,)), pltpu.SemaphoreType.REGULAR, dma((150,)), dma((150,))],
         compiler_params=pltpu.CompilerParams(vmem_limit_bytes=67_043_328, collective_id=1, has_side_effects=True),
         cost_estimate=pl.CostEstimate(flops=8 * tokens * model_width * ff_width, bytes_accessed=20_000_000, transcendentals=2 * tokens * ff_width),
         name="gather_forward",

time: 556 us -> 556 us (level)
  no operation moved by 1% of the time
where the time goes in v6:
time: 556 us
  Pallas kernels  532 us (96%)
  other arithmetic  11.4 us (2%)
  local copies, waits for them, and re-layouts  11 us (2%)
    pallas_call x1, Pallas kernels, backward_grads(): pl.pallas_call(functools.partial(backward_kernel, n_steps, n_chunks, cols...  363 us
    pallas_call x1, Pallas kernels, forward_stack(): pl.pallas_call(forward_kernel, in_specs=[hbm] * 5, out_specs=hbm, out_sha...  169 us

profile of v6, /device:TPU:0, one launch (start us, length us, event | category | flops | bytes accessed | tf_op | source)
XLA Modules:
  0.0 556.1 jit_solution(18216773069825615613)
XLA Ops:
  0.6 362.8 %backward_reduce.1 = (f32[2,64,4096]{2,1,0:T(8,128)}, f32[2,256,1024]{2,1,0:T(8,128)}, f32[8,128]{1,0:T(8,128)}) custom-call(bf16[2,3072,1024]{2,1,0:T(8,128)(2,1)} %bitcast.25, bf16[3072,1024]{1,0:T(8,128)(2,1)} %bitcast.26, bf16[2,1024,4096]{2,1,0:T(8,128)(2,1)} %w1_hbm.1, bf16[2,16,8,32,1024]{4,3,2,1,0:T(8,128)(2,1)} %bitcast.24, ...), custom_call_target="tpu_custom_call" | custom-call | flops 231928233984 | bytes 60000000 | tf_op jit(solution)/shard_map/backward_reduce/pallas_call | solution.py:340
  363.4 1.2 slice.17
  365.3 0.0 copy-start.2
  365.3 0.0 copy-start.3
  365.3 7.5 %fusion.4 = (bf16[2,64,4096]{2,1,0:T(8,128)(2,1)S(1)}, f32[2,64,4096]{2,1,0:T(8,128)}, f32[2,64,4096]{2,1,0:T(8,128)}, f32[2,64,4096]{2,1,0:T(8,128)}) fusion(f32[2,64,4096]{2,1,0:T(8,128)} %param.20, f32[2,64,4096]{2,1,0:T(8,128)} %get-tuple-element.10, f32[]{:T(128)} %bitcast.4, f32[2,64,4096]{2,1,0:T(8,128)} %param.22, f32[2,64,4096]{2,1,0:T(8,128)} %param.24), kind=kLoop, calls=%fused_computation.12 | loop fusion | flops 8912896 | bytes 15728644 | tf_op jit(solution)/shard_map/convert_element_type | solution.py:545
  372.9 0.0 copy-start
  372.9 0.0 copy-start.1
  372.9 0.1 copy.23
  372.9 1.1 fusion.6
  374.0 0.0 copy-done.2
  374.0 0.0 copy-done.3
  374.0 0.8 copy-done
  374.8 0.6 copy-done.1
  375.5 3.9 fusion.2
  379.4 1.0 slice_bitcast_fusion
  380.4 169.5 %gather_forward.1 = bf16[3072,1024]{1,0:T(8,128)(2,1)} custom-call(bf16[3072,1024]{1,0:T(8,128)(2,1)} %bitcast.27, bf16[256,1024]{1,0:T(8,128)(2,1)} %bitcast.23, bf16[256,1024]{1,0:T(8,128)(2,1)} %get-tuple-element.22.down0_hbm, bf16[256,1024]{1,0:T(8,128)(2,1)} %bitcast.22, bf16[256,1024]{1,0:T(8,128)(2,1)} %get-tuple-element.21.down1_hbm), custom_call_target="tpu_custom_call" | custom-call | flops 103079215104 | bytes 20000000 | tf_op jit(solution)/shard_map/gather_forward/pallas_call | solution.py:523
  549.9 6.2 %copy.25 = bf16[2,1536,1024]{2,1,0:T(8,128)(2,1)} copy(bf16[2,1536,1024]{2,1,0:T(8,128)(2,1)} %bitcast.19) | data formatting | bytes 12582912
Async XLA Ops:
  365.3 8.7 %copy-start.2 = (f32[2,256,1024]{2,1,0:T(8,128)S(1)}, f32[2,256,1024]{2,1,0:T(8,128)}, u32[]{:S(2)}) copy-start(f32[2,256,1024]{2,1,0:T(8,128)} %param.25) | copy-start | bytes 6291460
  365.3 8.7 %copy-start.3 = (f32[2,256,1024]{2,1,0:T(8,128)S(1)}, f32[2,256,1024]{2,1,0:T(8,128)}, u32[]{:S(2)}) copy-start(f32[2,256,1024]{2,1,0:T(8,128)} %get-tuple-element.12) | copy-start | bytes 6291460
  372.9 2.0 copy-start
  372.9 2.6 copy-start.1
